TPU v7x, 32 devices: a whole 2x2x4 slice. The times are simulated.
32 devices in a mesh: row: 4 (over y, x), col: 8 (over z, core).
Axes of the slice: x: 2, y: 2, z: 4, core: 2. Of those that a mesh axis runs over, the one named last changes fastest.
Arguments:
- coeffs: bfloat16 [16384, 2048], P('row'), may hold values from -1 to 1
- p_slots: int32 [4, 8, 64], P('row', 'col'), may hold values from 0 to 511, as said below
- p_count: int32 [4, 8], P('row', 'col'), may hold values from 1 to 64
- s_blocks: bfloat16 [4, 8, 64, 128, 128], P('row', 'col'), may hold values from -0.3984375 to 0.3984375
- s_slots: int32 [4, 8, 64], P('row', 'col'), may hold values from 0 to 511, as said below
- s_count: int32 [4, 8], P('row', 'col'), may hold values from 1 to 64
- q_slots: int32 [4, 8, 64], P('row', 'col'), may hold values from 0 to 511, as said below
- q_count: int32 [4, 8], P('row', 'col'), may hold values from 1 to 64
Outputs:
- density: bfloat16 [4, 8, 64, 128, 128], P('row', 'col')
- product: float32 [4, 8, 64, 128, 128], P('row', 'col')
Inputs may be any that keep to these rules, and one draw needn't show every extreme that they name: `p_slots`: on each device the live slots name different blocks of its tile; at least one device has all 64 slots live, which one is drawn. `s_slots`: on each device the live slots name different positions; at least one device has all 64 slots live, which one is drawn. `q_slots`: on each device the live slots name different blocks of its tile; at least one device has all 64 slots live, which one is drawn.
All inputs are finite; a program needn't handle non-finite values.
Results may differ from a plain program's by a relative error of at most 0.0029.
Values may be sent and summed in bfloat16 or wider, within the bound.
A program may use at most 192 MiB of HBM per device.

v0:
```python
import functools

import jax
import jax.numpy as jnp
from jax import lax
from jax.experimental import pallas as pl
from jax.experimental.pallas import tpu as pltpu
from jax.sharding import PartitionSpec as P

MESH = pl.DeviceIdType.MESH
MIB = 1 << 20


def rows_kernel(rows_n, cols_n, coeffs, out, send, recv):
    row, col = lax.axis_index("row"), lax.axis_index("col")
    sub = cols_n // rows_n
    height = out.shape[0]
    piece = height // rows_n
    half, share = lax.rem(col, sub), lax.div(col, sub)
    owner = lax.div(col, sub)
    targets = [
        {"row": lax.rem(row + step, rows_n), "col": row * sub + half} for step in range(1, rows_n)
    ]
    sources = [{"row": owner, "col": part * sub + half} for part in range(rows_n)]
    barrier = pltpu.get_barrier_semaphore()
    for device in targets:
        pl.semaphore_signal(barrier, inc=1, device_id=device, device_id_type=MESH)

    @pl.when(row != owner)
    def _():
        for device in sources:
            pl.semaphore_signal(barrier, inc=1, device_id=device, device_id_type=MESH)

    pl.semaphore_wait(barrier, rows_n - 1 + jnp.where(row != owner, rows_n, 0))

    def copy(step, part, device):
        start = half * height + share * piece
        return pltpu.make_async_remote_copy(
            src_ref=coeffs.at[pl.ds(pl.multiple_of(start, piece), piece)],
            dst_ref=out.at[pl.ds(pl.multiple_of(part * piece, piece), piece)],
            send_sem=send.at[step],
            recv_sem=recv.at[part],
            device_id=device,
            device_id_type=MESH,
        )

    sends = [copy(step, share, device) for step, device in enumerate(targets)]
    for one in sends:
        one.start()

    @pl.when(row != owner)
    def _():
        for part, device in enumerate(sources):
            copy(0, part, device).wait_recv()

    for one in sends:
        one.wait_send()


def square_kernel(rows_n, cols_n, parts, coeffs, out, send, recv):
    row, col = lax.axis_index("row"), lax.axis_index("col")
    sub = cols_n // rows_n
    height = out.shape[0]
    size = height // (2 * parts)
    owner = lax.div(col, sub)
    first = lax.rem(col, sub) * height
    y, x = lax.div(row, 2), lax.rem(row, 2)
    dy = lax.rem(y + lax.div(owner, 2), 2)
    dx = lax.rem(x + lax.rem(owner, 2), 2)
    along_x, along_y = y * 2 + 1 - x, (1 - y) * 2 + x
    is_source = row == owner
    sends = [jnp.logical_or(dx == 1, dy == 0), jnp.logical_or(dx == 0, dy == 1)]
    following = [
        jnp.where(dx == dy, along_x, along_y),
        jnp.where(dx == dy, along_y, along_x),
    ]

    barrier = pltpu.get_barrier_semaphore()
    for near in (along_x, along_y):
        pl.semaphore_signal(
            barrier, inc=1, device_id={"row": near, "col": col}, device_id_type=MESH
        )
    pl.semaphore_wait(barrier, 2)

    def copy(way, part, from_input):
        offset = (way * parts + part) * size
        where = out.at[pl.ds(offset, size)]
        start = pl.multiple_of(first + offset, size)
        return pltpu.make_async_remote_copy(
            src_ref=coeffs.at[pl.ds(start, size)] if from_input else where,
            dst_ref=where,
            send_sem=send.at[way, part],
            recv_sem=recv.at[way, part],
            device_id={"row": following[way], "col": col},
            device_id_type=MESH,
        )

    @pl.when(is_source)
    def _():
        for part in range(parts):
            for way in range(2):
                copy(way, part, True).start()

    @pl.when(jnp.logical_not(is_source))
    def _():
        for part in range(parts):
            for way in range(2):
                copy(way, part, False).wait_recv()
                pl.when(sends[way])(lambda: copy(way, part, False).start())

    for way in range(2):

        @pl.when(sends[way])
        def _():
            for part in range(parts):
                copy(way, part, False).wait_send()


def gather_rows(coeffs, rows_n, cols_n):
    height = coeffs.shape[0] * rows_n // cols_n
    if rows_n == 4:
        parts = max(1, height // 256)
        body = functools.partial(square_kernel, rows_n, cols_n, parts)
        sems = [pltpu.SemaphoreType.DMA((2, parts))] * 2
    else:
        body = functools.partial(rows_kernel, rows_n, cols_n)
        sems = [pltpu.SemaphoreType.DMA((rows_n - 1,)), pltpu.SemaphoreType.DMA((rows_n,))]
    return pl.pallas_call(
        body,
        out_shape=jax.ShapeDtypeStruct((height, coeffs.shape[1]), coeffs.dtype),
        in_specs=[pl.BlockSpec(memory_space=pl.ANY)],
        out_specs=pl.BlockSpec(memory_space=pl.ANY),
        scratch_shapes=sems,
        compiler_params=pltpu.CompilerParams(collective_id=0, has_side_effects=True),
    )(coeffs)


def density_kernel(rows_n, cols_n, ids, count, coeffs, others, out, left, right, sem):
    row, col = lax.axis_index("row"), lax.axis_index("col")
    sub = cols_n // rows_n
    height = others.shape[0]
    tile_cols = height // 128
    load_left = pltpu.make_async_copy(coeffs, left, sem.at[0])
    load_left.start()
    here = row == lax.div(col, sub)
    start = pl.multiple_of(lax.rem(col, sub) * height, height)
    load_own = pltpu.make_async_copy(coeffs.at[pl.ds(start, height)], right, sem.at[1])
    load_other = pltpu.make_async_copy(others, right, sem.at[1])

    @pl.when(here)
    def _():
        load_own.start()

    @pl.when(jnp.logical_not(here))
    def _():
        load_other.start()

    live = count[0]
    load_left.wait()
    load_other.wait()

    def block(slot, carry):
        a = pl.multiple_of(lax.div(ids[slot], tile_cols) * 128, 128)
        b = pl.multiple_of(lax.rem(ids[slot], tile_cols) * 128, 128)
        raw = lax.dot_general(
            left[pl.ds(a, 128), :],
            right[pl.ds(b, 128), :],
            (((1,), (1,)), ((), ())),
            preferred_element_type=jnp.float32,
        )
        out[slot] = raw.astype(out.dtype)
        return carry

    def clear(slot, carry):
        out[slot] = jnp.zeros(out.shape[1:], out.dtype)
        return carry

    lax.fori_loop(0, live, block, 0)
    lax.fori_loop(live, out.shape[0], clear, 0)


def density(ids, count, coeffs, others, rows_n, cols_n):
    slots = ids.shape[0]
    return pl.pallas_call(
        functools.partial(density_kernel, rows_n, cols_n),
        out_shape=jax.ShapeDtypeStruct((slots, 128, 128), jnp.bfloat16),
        in_specs=[pl.BlockSpec(memory_space=pltpu.SMEM)] * 2
        + [pl.BlockSpec(memory_space=pl.ANY)] * 2,
        out_specs=pl.BlockSpec(memory_space=pltpu.VMEM),
        scratch_shapes=[
            pltpu.VMEM(coeffs.shape, coeffs.dtype),
            pltpu.VMEM(others.shape, coeffs.dtype),
            pltpu.SemaphoreType.DMA((2,)),
        ],
        compiler_params=pltpu.CompilerParams(vmem_limit_bytes=40 * MIB),
    )(ids, count, coeffs, others)


def blocks_kernel(rows_n, cols_n, parts, p_own, s_own, p_all, s_all, *sems):
    send, recv, pass_send, pass_recv, s_send, s_recv = sems
    row, col = lax.axis_index("row"), lax.axis_index("col")
    length = cols_n // 2
    z, core = lax.div(col, 2), lax.rem(col, 2)
    size = p_own.shape[0] // parts
    right, left = {"row": row, "col": col + 2}, {"row": row, "col": col - 2}
    partner = {"row": row, "col": z * 2 + 1 - core}
    column = [{"row": lax.rem(row + step, rows_n), "col": col} for step in range(1, rows_n)]
    has_right, has_left = z + 1 < length, z > 0

    barrier = pltpu.get_barrier_semaphore()

    def greet(device):
        pl.semaphore_signal(barrier, inc=1, device_id=device, device_id_type=MESH)

    greet(partner)
    for device in column:
        greet(device)

    @pl.when(has_right)
    def _():
        greet(right)

    @pl.when(has_left)
    def _():
        greet(left)

    pl.semaphore_wait(barrier, rows_n + jnp.where(has_right, 1, 0) + jnp.where(has_left, 1, 0))

    def remote(src, dst, send_sem, recv_sem, device):
        return pltpu.make_async_remote_copy(
            src_ref=src,
            dst_ref=dst,
            send_sem=send_sem,
            recv_sem=recv_sem,
            device_id=device,
            device_id_type=MESH,
        )

    def piece(source, lane, part):
        return p_all.at[source * 2 + lane, pl.ds(part * size, size)]

    def origin(way, step):
        return z - step if way == 0 else z + step

    def sent(way, step, part):
        where = piece(origin(way, step), core, part)
        src = p_own.at[pl.ds(part * size, size)] if step == 0 else where
        device = right if way == 0 else left
        return remote(src, where, send.at[way, step, part], recv.at[way, step, part], device)

    def passed(way, step, part):
        where = piece(origin(way, step), core, part)
        src = p_own.at[pl.ds(part * size, size)] if step == 0 else where
        return remote(
            src, where, pass_send.at[way, step, part], pass_recv.at[way, step, part], partner
        )

    def onward(way):
        return has_right if way == 0 else has_left

    def exists(way, step):
        return z >= step if way == 0 else z + step < length

    for part in range(parts):
        for way in range(2):
            pl.when(onward(way))(lambda way=way: sent(way, 0, part).start())
    s_sends = [
        remote(s_own, s_all.at[row], s_send.at[n], s_recv.at[n], device)
        for n, device in enumerate(column)
    ]
    for one in s_sends:
        one.start()
    for part in range(parts):
        passed(0, 0, part).start()
    for step in range(1, length):
        for part in range(parts):
            for way in range(2):

                @pl.when(exists(way, step))
                def _():
                    sent(way, step - 1, part).wait_recv()
                    passed(way, step, part).start()
                    if step < length - 1:
                        pl.when(onward(way))(lambda: sent(way, step, part).start())

    for part in range(parts):
        passed(0, 0, part).wait()
        for way in range(2):
            pl.when(onward(way))(lambda way=way: sent(way, 0, part).wait_send())
    for step in range(1, length):
        for part in range(parts):
            for way in range(2):

                @pl.when(exists(way, step))
                def _():
                    passed(way, step, part).wait()
                    if step < length - 1:
                        pl.when(onward(way))(lambda: sent(way, step, part).wait_send())

    for one in s_sends:
        one.wait()


def gather_blocks(p_own, s_own, rows_n, cols_n):
    parts = 4 if p_own.shape[0] % 4 == 0 else 1
    table = pltpu.SemaphoreType.DMA((2, cols_n // 2, parts))
    return pl.pallas_call(
        functools.partial(blocks_kernel, rows_n, cols_n, parts),
        out_shape=(
            jax.ShapeDtypeStruct((cols_n,) + p_own.shape, p_own.dtype),
            jax.ShapeDtypeStruct((rows_n,) + s_own.shape, s_own.dtype),
        ),
        in_specs=[pl.BlockSpec(memory_space=pl.ANY)] * 2,
        out_specs=[pl.BlockSpec(memory_space=pl.ANY)] * 2,
        scratch_shapes=[table] * 4 + [pltpu.SemaphoreType.DMA((rows_n - 1,))] * 2,
        compiler_params=pltpu.CompilerParams(collective_id=1, has_side_effects=True),
    )(p_own, s_own)


def product_kernel(rows_n, cols_n, codes, counts, p_own, s_own, p_all, s_all, out, left, right, sem):
    row, col = lax.axis_index("row"), lax.axis_index("col")
    p_max, s_max = p_own.shape[0], s_own.shape[0]
    base = rows_n * s_max
    loads = [pltpu.make_async_copy(p_own, left.at[pl.ds(col * p_max, p_max)], sem.at[0])]
    loads += [pltpu.make_async_copy(s_own, right.at[pl.ds(row * s_max, s_max)], sem.at[1])]
    for step in range(1, cols_n):
        at = lax.rem(col + step, cols_n)
        loads += [
            pltpu.make_async_copy(
                p_all.at[at], left.at[pl.ds(at * p_max, p_max)], sem.at[len(loads)]
            )
        ]
    for step in range(1, rows_n):
        at = lax.rem(row + step, rows_n)
        loads += [
            pltpu.make_async_copy(
                s_all.at[at], right.at[pl.ds(at * s_max, s_max)], sem.at[len(loads)]
            )
        ]
    for load in loads:
        load.start()
    for load in loads:
        load.wait()

    def slot(q, carry):
        def term(n, total):
            code = codes[q, n]
            return total + jnp.dot(
                left[lax.div(code, base)],
                right[lax.rem(code, base)],
                preferred_element_type=jnp.float32,
            )

        out[q] = lax.fori_loop(0, counts[q], term, jnp.zeros((128, 128), jnp.float32))
        return carry

    lax.fori_loop(0, out.shape[0], slot, 0)


def block_product(codes, counts, p_own, s_own, p_all, s_all):
    cols_n, p_max = p_all.shape[:2]
    rows_n, s_max = s_all.shape[:2]
    return pl.pallas_call(
        functools.partial(product_kernel, rows_n, cols_n),
        out_shape=jax.ShapeDtypeStruct((counts.shape[0], 128, 128), jnp.float32),
        in_specs=[pl.BlockSpec(memory_space=pltpu.SMEM)] * 2
        + [pl.BlockSpec(memory_space=pl.ANY)] * 4,
        out_specs=pl.BlockSpec(memory_space=pltpu.VMEM),
        scratch_shapes=[
            pltpu.VMEM((cols_n * p_max, 128, 128), p_all.dtype),
            pltpu.VMEM((rows_n * s_max, 128, 128), s_all.dtype),
            pltpu.SemaphoreType.DMA((cols_n + rows_n,)),
        ],
        compiler_params=pltpu.CompilerParams(vmem_limit_bytes=40 * MIB),
    )(codes, counts, p_own, s_own, p_all, s_all)


def match_lists(p_codes, s_codes, q_ids, q_live, tile_cols, span):
    cols_n, p_max = p_codes.shape
    rows_n, s_max = s_codes.shape
    q_row, q_col = q_ids // tile_cols, q_ids % tile_cols
    at = jnp.arange(tile_cols, dtype=jnp.int32)
    p_want = q_row[:, None] * tile_cols + at[None, :]
    p_hit = p_codes[None, :, None, :] == p_want[:, None, :, None]
    p_slot = jnp.arange(cols_n * p_max, dtype=jnp.int32).reshape(1, cols_n, 1, p_max)
    p_at = jnp.max(jnp.where(p_hit, p_slot, -1), axis=3)
    level = jnp.arange(span * tile_cols, dtype=jnp.int32).reshape(span, tile_cols)
    s_want = level[None] * tile_cols + q_col[:, None, None]
    s_hit = s_codes[None, None, :, None, :] == s_want[:, :, None, :, None]
    s_slot = jnp.arange(rows_n * s_max, dtype=jnp.int32).reshape(1, 1, rows_n, 1, s_max)
    s_at = jnp.max(jnp.where(s_hit, s_slot, -1), axis=4)
    p_at = p_at.reshape(q_ids.shape[0], -1)
    s_at = s_at.reshape(q_ids.shape[0], -1)
    depth = p_at.shape[1]
    match = (p_at >= 0) & (s_at >= 0) & q_live[:, None]
    code = jnp.where(match, p_at * (rows_n * s_max) + s_at, 0)
    order = jnp.arange(depth, dtype=jnp.int32)
    before = order[None, :, None] > order[None, None, :]
    rank = jnp.sum((before & match[:, None, :]).astype(jnp.int32), axis=2)
    rank = jnp.where(match, rank, -1)
    picked = rank[:, None, :] == order[None, :, None]
    codes = jnp.sum(jnp.where(picked, code[:, None, :], 0), axis=2)
    return codes, jnp.sum(match.astype(jnp.int32), axis=1)


def on_device(coeffs, p_slots, p_count, s_blocks, s_slots, s_count, q_slots, q_count):
    rows_n = lax.axis_size("row")
    cols_n = lax.axis_size("col")
    tile_cols = coeffs.shape[0] * rows_n // cols_n // 128
    p_ids, s_ids, q_ids = p_slots[0, 0], s_slots[0, 0], q_slots[0, 0]
    s_own = s_blocks[0, 0]
    p_max, s_max, q_max = p_ids.shape[0], s_ids.shape[0], q_ids.shape[0]

    def live(ids, count):
        return jnp.arange(ids.shape[0], dtype=jnp.int32) < count[0, 0]

    p_codes = lax.all_gather(jnp.where(live(p_ids, p_count), p_ids, -1), "col")
    s_codes = lax.all_gather(jnp.where(live(s_ids, s_count), s_ids, -1), "row")
    codes, counts = match_lists(
        p_codes, s_codes, q_ids, live(q_ids, q_count), tile_cols, cols_n // rows_n
    )
    others = gather_rows(coeffs, rows_n, cols_n)
    p_own = density(p_ids, p_count[0], coeffs, others, rows_n, cols_n)
    p_all, s_all = gather_blocks(p_own, s_own, rows_n, cols_n)
    product = block_product(codes, counts, p_own, s_own, p_all, s_all)
    return (p_own.reshape(1, 1, p_max, 128, 128), product.reshape(1, 1, q_max, 128, 128))


def solution(mesh):
    return jax.shard_map(
        on_device,
        mesh=mesh,
        in_specs=(
            P("row", None),
            P("row", "col", None),
            P("row", "col"),
            P("row", "col", None, None, None),
            P("row", "col", None),
            P("row", "col"),
            P("row", "col", None),
            P("row", "col"),
        ),
        out_specs=(P("row", "col", None, None, None), P("row", "col", None, None, None)),
        check_vma=False,
    )
```

profile of v0, /device:TPU:1, one launch (start us, length us, event | category | flops | bytes accessed | tf_op | source)
XLA Modules:
  0.0 526.8 jit_solution(1789970472036976143)
XLA Ops:
  2.6 0.7 fusion.1
  3.2 0.7 fusion
  3.9 0.7 and_select_fusion
  4.6 6.7 %all-gather.1 = s32[4,1,64]{2,1,0:T(1,128)S(1)} all-gather(s32[1,1,64]{2,1,0:T(1,128)S(1)} %fusion.1), channel_id=1, replica_groups=mesh['row'=4,'col'=8] {'row'}, dimensions={0}, use_global_device_ids=true | all-gather | bytes 1280 | tf_op jit(solution)/shard_map/all_gather | solution.py:418
  11.3 14.5 %all-gather = s32[8,1,64]{2,1,0:T(1,128)S(1)} all-gather(s32[1,1,64]{2,1,0:T(1,128)S(1)} %fusion), channel_id=1, replica_groups=mesh['row'=4,'col'=8] {'col'}, dimensions={0}, use_global_device_ids=true | all-gather | bytes 2304 | tf_op jit(solution)/shard_map/all_gather | solution.py:417
  25.8 0.1 iota_add_fusion
  25.9 0.1 broadcast_add_fusion
  26.1 9.4 %select_reduce_fusion.1 = s32[64,2,4,16]{3,2,1,0:T(4,128)S(1)} fusion(s32[4,64]{1,0:T(4,128)S(1)} %multiply_add_fusion.1, s32[64,2,16]{2,1,0:T(2,128)S(1)} %broadcast_add_fusion, s32[4,64]{1,0:T(4,128)S(1)} %bitcast.53), kind=kLoop, calls=%fused_computation.3 | loop fusion | flops 1564672 | bytes 43008 | tf_op jit(solution)/shard_map/reduce_max | solution.py:391
  35.4 0.1 copy.24
  35.5 0.1 copy.25
  35.6 8.9 %select_reduce_fusion.2 = s32[64,8,16]{2,1,0:T(8,128)S(1)} fusion(s32[8,64]{1,0:T(8,128)S(1)} %multiply_add_fusion, s32[64,16]{1,0:T(8,128)S(1)} %iota_add_fusion, s32[8,64]{1,0:T(8,128)S(1)} %bitcast.52), kind=kLoop, calls=%fused_computation.4 | loop fusion | flops 1564672 | bytes 40960 | tf_op jit(solution)/shard_map/reduce_max | solution.py:386
  44.6 0.1 copy.27
  44.7 0.1 copy.28
  44.8 1.3 convert_reduce_fusion.1.counts
  46.1 0.1 copy.23
  46.2 0.1 copy.26
  46.4 0.1 add_select_fusion
  46.4 1.4 convert_reduce_fusion
  47.8 1.7 select_reduce_fusion.codes
  49.5 0.0 copy-start.4
  49.5 91.6 %shard_map.95.others = bf16[2048,2048]{1,0:T(8,128)(2,1)} custom-call(bf16[4096,2048]{1,0:T(8,128)(2,1)} %coeffs.3), custom_call_target="tpu_custom_call" | custom-call | tf_op jit(solution)/shard_map/pallas_call | solution.py:128
  141.2 0.0 copy-done.4
  141.2 0.0 copy-start
  141.2 3.4 copy-done
  144.6 28.9 %shard_map.96.p_own = bf16[64,128,128]{2,1,0:T(8,128)(2,1)} custom-call(s32[64]{0:T(128)S(1)} %bitcast.46, s32[1]{0:T(128)} %bitcast.39.count, bf16[4096,2048]{1,0:T(8,128)(2,1)} %coeffs.3, bf16[2048,2048]{1,0:T(8,128)(2,1)S(1)} %copy-done), custom_call_target="tpu_custom_call" | custom-call | tf_op jit(solution)/shard_map/pallas_call | solution.py:184
  173.5 0.0 copy-start.1
  173.6 337.0 %shard_map.97 = (bf16[8,64,128,128]{3,2,1,0:T(8,128)(2,1)}, bf16[4,64,128,128]{3,2,1,0:T(8,128)(2,1)}) custom-call(bf16[64,128,128]{2,1,0:T(8,128)(2,1)} %shard_map.96.p_own, bf16[64,128,128]{2,1,0:T(8,128)(2,1)} %bitcast.44), custom_call_target="tpu_custom_call" | custom-call | tf_op jit(solution)/shard_map/pallas_call | solution.py:307
  510.5 0.0 copy-done.1
  510.6 0.0 copy-start.2
  510.6 3.4 copy-done.2
  513.9 0.0 copy-start.3
  513.9 1.6 copy-done.3
  515.5 11.1 %shard_map.98 = f32[64,128,128]{2,1,0:T(8,128)} custom-call(s32[64,128]{1,0:T(8,128)S(1)} %select_reduce_fusion.codes, s32[64]{0:T(128)S(1)} %convert_reduce_fusion.1.counts, bf16[64,128,128]{2,1,0:T(8,128)(2,1)S(1)} %copy-done.1, bf16[64,128,128]{2,1,0:T(8,128)(2,1)S(1)} %bitcast.45, bf16[8,64,128,128]{3,2,1,0:T(8,128)(2,1)} %get-tuple-element.4.p_all, ...), custom_call_target="tpu_custom_call" | custom-call | tf_op jit(solution)/shard_map/pallas_call | solution.py:363
  (8 shorter events, 0.1 us)
Async XLA Ops:
  49.5 91.7 %copy-start.4 = (s32[1,1,64]{2,1,0:T(1,128)S(1)}, s32[1,1,64]{2,1,0:T(1,128)}, u32[]{:S(2)}) copy-start(s32[1,1,64]{2,1,0:T(1,128)} %param.9) | copy-start | bytes 772
  141.2 3.4 copy-start
  173.5 337.0 %copy-start.1 = (bf16[64,128,128]{2,1,0:T(8,128)(2,1)S(1)}, bf16[64,128,128]{2,1,0:T(8,128)(2,1)}, u32[]{:S(2)}) copy-start(bf16[64,128,128]{2,1,0:T(8,128)(2,1)} %shard_map.96.p_own) | copy-start | bytes 6291460
  510.6 3.4 copy-start.2
  513.9 1.6 copy-start.3
where the time goes:
time: 536 us; the launch traced here: 527 us
  Pallas kernels  469 us (88%)
  other arithmetic  25 us (5%)
  blocking collectives  21.2 us (4%)
  local copies, waits for them, and re-layouts  8.99 us (2%)
    pallas_call x1, Pallas kernels, gather_blocks(): pl.pallas_call(functools.partial(blocks_kernel, rows_n, cols_n, parts), o...  337 us
    pallas_call x1, Pallas kernels, gather_rows(): pl.pallas_call(body, out_shape=jax.ShapeDtypeStruct((height, coeffs.shape...  91.6 us
    pallas_call x1, Pallas kernels, density(): pl.pallas_call(functools.partial(density_kernel, rows_n, cols_n), out_sha...  28.9 us
    all_gather x1, blocking collectives, on_device(): p_codes = lax.all_gather(jnp.where(live(p_ids, p_count), p_ids, -1), 'col')  14.5 us
    pallas_call x1, Pallas kernels, block_product(): pl.pallas_call(functools.partial(product_kernel, rows_n, cols_n), out_sha...  11.1 us

commit v1 on v0

--- a/solution.py
+++ b/solution.py
@@ -9,6 +9,9 @@
 
 MESH = pl.DeviceIdType.MESH
 MIB = 1 << 20
+CHUNK = 256
+PIECE = 2
+DEPTH = 3
 
 
 def rows_kernel(rows_n, cols_n, coeffs, out, send, recv):
@@ -57,74 +60,10 @@
         one.wait_send()
 
 
-def square_kernel(rows_n, cols_n, parts, coeffs, out, send, recv):
-    row, col = lax.axis_index("row"), lax.axis_index("col")
-    sub = cols_n // rows_n
-    height = out.shape[0]
-    size = height // (2 * parts)
-    owner = lax.div(col, sub)
-    first = lax.rem(col, sub) * height
-    y, x = lax.div(row, 2), lax.rem(row, 2)
-    dy = lax.rem(y + lax.div(owner, 2), 2)
-    dx = lax.rem(x + lax.rem(owner, 2), 2)
-    along_x, along_y = y * 2 + 1 - x, (1 - y) * 2 + x
-    is_source = row == owner
-    sends = [jnp.logical_or(dx == 1, dy == 0), jnp.logical_or(dx == 0, dy == 1)]
-    following = [
-        jnp.where(dx == dy, along_x, along_y),
-        jnp.where(dx == dy, along_y, along_x),
-    ]
-
-    barrier = pltpu.get_barrier_semaphore()
-    for near in (along_x, along_y):
-        pl.semaphore_signal(
-            barrier, inc=1, device_id={"row": near, "col": col}, device_id_type=MESH
-        )
-    pl.semaphore_wait(barrier, 2)
-
-    def copy(way, part, from_input):
-        offset = (way * parts + part) * size
-        where = out.at[pl.ds(offset, size)]
-        start = pl.multiple_of(first + offset, size)
-        return pltpu.make_async_remote_copy(
-            src_ref=coeffs.at[pl.ds(start, size)] if from_input else where,
-            dst_ref=where,
-            send_sem=send.at[way, part],
-            recv_sem=recv.at[way, part],
-            device_id={"row": following[way], "col": col},
-            device_id_type=MESH,
-        )
-
-    @pl.when(is_source)
-    def _():
-        for part in range(parts):
-            for way in range(2):
-                copy(way, part, True).start()
-
-    @pl.when(jnp.logical_not(is_source))
-    def _():
-        for part in range(parts):
-            for way in range(2):
-                copy(way, part, False).wait_recv()
-                pl.when(sends[way])(lambda: copy(way, part, False).start())
-
-    for way in range(2):
-
-        @pl.when(sends[way])
-        def _():
-            for part in range(parts):
-                copy(way, part, False).wait_send()
-
-
 def gather_rows(coeffs, rows_n, cols_n):
     height = coeffs.shape[0] * rows_n // cols_n
-    if rows_n == 4:
-        parts = max(1, height // 256)
-        body = functools.partial(square_kernel, rows_n, cols_n, parts)
-        sems = [pltpu.SemaphoreType.DMA((2, parts))] * 2
-    else:
-        body = functools.partial(rows_kernel, rows_n, cols_n)
-        sems = [pltpu.SemaphoreType.DMA((rows_n - 1,)), pltpu.SemaphoreType.DMA((rows_n,))]
+    body = functools.partial(rows_kernel, rows_n, cols_n)
+    sems = [pltpu.SemaphoreType.DMA((rows_n - 1,)), pltpu.SemaphoreType.DMA((rows_n,))]
     return pl.pallas_call(
         body,
         out_shape=jax.ShapeDtypeStruct((height, coeffs.shape[1]), coeffs.dtype),
@@ -194,6 +133,140 @@
         ],
         compiler_params=pltpu.CompilerParams(vmem_limit_bytes=40 * MIB),
     )(ids, count, coeffs, others)
+
+
+def panel_kernel(rows_n, cols_n, chunks, parts, depth, ids, count, coeffs, out, *scratch):
+    left, total, send, recv, sem = scratch[chunks:]
+    right = scratch[:chunks]
+    row, col = lax.axis_index("row"), lax.axis_index("col")
+    sub = cols_n // rows_n
+    tile_cols, _, wide = right[0].shape
+    size = tile_cols // (2 * parts)
+    owner = lax.div(col, sub)
+    first = lax.rem(col, sub) * tile_cols
+    y, x = lax.div(row, 2), lax.rem(row, 2)
+    dy = lax.rem(y + lax.div(owner, 2), 2)
+    dx = lax.rem(x + lax.rem(owner, 2), 2)
+    along_x, along_y = y * 2 + 1 - x, (1 - y) * 2 + x
+    is_source = row == owner
+    sends = [jnp.logical_or(dx == 1, dy == 0), jnp.logical_or(dx == 0, dy == 1)]
+    following = [
+        jnp.where(dx == dy, along_x, along_y),
+        jnp.where(dx == dy, along_y, along_x),
+    ]
+    steps = [(k, part) for k in range(chunks) for part in range(parts)]
+
+    def offset(way, part):
+        return (way * parts + part) * size
+
+    def load(way, k, part):
+        return pltpu.make_async_copy(
+            coeffs.at[pl.ds(first + offset(way, part), size), :, pl.ds(k * wide, wide)],
+            right[k].at[pl.ds(offset(way, part), size)],
+            recv.at[way, k * parts + part],
+        )
+
+    def copy(way, k, part):
+        where = right[k].at[pl.ds(offset(way, part), size)]
+        return pltpu.make_async_remote_copy(
+            src_ref=where,
+            dst_ref=where,
+            send_sem=send.at[way, k * parts + part],
+            recv_sem=recv.at[way, k * parts + part],
+            device_id={"row": following[way], "col": col},
+            device_id_type=MESH,
+        )
+
+    @pl.when(is_source)
+    def _():
+        for k, part in steps:
+            for way in range(2):
+                load(way, k, part).start()
+
+    load_left = pltpu.make_async_copy(coeffs, left, sem.at[0])
+    load_left.start()
+    barrier = pltpu.get_barrier_semaphore()
+    for near in (along_x, along_y):
+        pl.semaphore_signal(
+            barrier, inc=1, device_id={"row": near, "col": col}, device_id_type=MESH
+        )
+    pl.semaphore_wait(barrier, 2)
+    live = count[0]
+
+    def relay(k):
+        for part in range(parts):
+            now = k * parts + part
+            for way in range(2):
+
+                @pl.when(sends[way])
+                def _():
+                    copy(way, k, part).wait_recv()
+                    if now >= depth:
+                        copy(way, *steps[now - depth]).wait_send()
+                    copy(way, k, part).start()
+
+    relay(0)
+    load_left.wait()
+    for k in range(chunks):
+        if k < chunks - 1:
+            relay(k + 1)
+        for way in range(2):
+
+            @pl.when(jnp.logical_not(sends[way]))
+            def _():
+                for part in range(parts):
+                    copy(way, k, part).wait_recv()
+
+        def block(slot, carry, k=k):
+            raw = lax.dot_general(
+                left[lax.div(ids[slot], tile_cols), :, pl.ds(k * wide, wide)],
+                right[k][lax.rem(ids[slot], tile_cols)],
+                (((1,), (1,)), ((), ())),
+                preferred_element_type=jnp.float32,
+            )
+            if k > 0:
+                raw = raw + total[slot]
+            if k < chunks - 1:
+                total[slot] = raw
+            else:
+                out[slot] = jnp.where(slot < live, raw, 0.0).astype(out.dtype)
+            return carry
+
+        lax.fori_loop(0, out.shape[0], block, 0, unroll=4)
+
+    for way in range(2):
+
+        @pl.when(sends[way])
+        def _():
+            for k, part in steps[-depth:]:
+                copy(way, k, part).wait_send()
+
+
+def panel_density(ids, count, coeffs, rows_n, cols_n):
+    slots = ids.shape[0]
+    orbitals = coeffs.shape[1]
+    blocks = coeffs.reshape(-1, 128, orbitals)
+    tile_cols = blocks.shape[0] * rows_n // cols_n
+    chunks = max(1, orbitals // CHUNK)
+    parts = max(1, tile_cols // (2 * PIECE))
+    return pl.pallas_call(
+        functools.partial(panel_kernel, rows_n, cols_n, chunks, parts, DEPTH),
+        out_shape=jax.ShapeDtypeStruct((slots, 128, 128), jnp.bfloat16),
+        in_specs=[pl.BlockSpec(memory_space=pltpu.SMEM)] * 2
+        + [pl.BlockSpec(memory_space=pl.ANY)],
+        out_specs=pl.BlockSpec(memory_space=pltpu.VMEM),
+        scratch_shapes=[pltpu.VMEM((tile_cols, 128, orbitals // chunks), coeffs.dtype)] * chunks
+        + [
+            pltpu.VMEM(blocks.shape, coeffs.dtype),
+            pltpu.VMEM((slots, 128, 128), jnp.float32),
+            pltpu.SemaphoreType.DMA((2, chunks * parts)),
+            pltpu.SemaphoreType.DMA((2, chunks * parts)),
+            pltpu.SemaphoreType.DMA((1,)),
+        ],
+        compiler_params=pltpu.CompilerParams(
+            collective_id=2, has_side_effects=True, vmem_limit_bytes=40 * MIB
+        ),
+    )(ids, count, blocks)
 
 
 def blocks_kernel(rows_n, cols_n, parts, p_own, s_own, p_all, s_all, *sems):
@@ -419,8 +492,11 @@
     codes, counts = match_lists(
         p_codes, s_codes, q_ids, live(q_ids, q_count), tile_cols, cols_n // rows_n
     )
-    others = gather_rows(coeffs, rows_n, cols_n)
-    p_own = density(p_ids, p_count[0], coeffs, others, rows_n, cols_n)
+    if rows_n == 4:
+        p_own = panel_density(p_ids, p_count[0], coeffs, rows_n, cols_n)
+    else:
+        others = gather_rows(coeffs, rows_n, cols_n)
+        p_own = density(p_ids, p_count[0], coeffs, others, rows_n, cols_n)
     p_all, s_all = gather_blocks(p_own, s_own, rows_n, cols_n)
     product = block_product(codes, counts, p_own, s_own, p_all, s_all)
     return (p_own.reshape(1, 1, p_max, 128, 128), product.reshape(1, 1, q_max, 128, 128))

time: 536 us -> 317 us (0.59)
  the two profiles are of different devices: /device:TPU:1 before, /device:TPU:0 now
where the time goes in v1:
time: 317 us; the launch traced here: 315 us
  Pallas kernels  257 us (81%)
  other arithmetic  24.6 us (8%)
  blocking collectives  21.6 us (7%)
  local copies, waits for them, and re-layouts  8.9 us (3%)
    pallas_call x1, Pallas kernels, gather_blocks(): pl.pallas_call(functools.partial(blocks_kernel, rows_n, cols_n, parts), o...  152 us
    pallas_call x1, Pallas kernels, panel_density(): pl.pallas_call(functools.partial(panel_kernel, rows_n, cols_n, chunks, pa...  93.3 us
    all_gather x1, blocking collectives, on_device(): p_codes = lax.all_gather(jnp.where(live(p_ids, p_count), p_ids, -1), 'col')  13.4 us
    pallas_call x1, Pallas kernels, block_product(): pl.pallas_call(functools.partial(product_kernel, rows_n, cols_n), out_sha...  11.9 us
    reduce_max x1, other arithmetic, match_lists(): s_at = jnp.max(jnp.where(s_hit, s_slot, -1), axis=4)  9.17 us
    reduce_max x1, other arithmetic, match_lists(): p_at = jnp.max(jnp.where(p_hit, p_slot, -1), axis=3)  8.85 us
    unnamed x11, local copies, waits for them, and re-layouts  8.26 us
    all_gather x1, blocking collectives, on_device(): s_codes = lax.all_gather(jnp.where(live(s_ids, s_count), s_ids, -1), 'row')  8.12 us

profile of v1, /device:TPU:0, one launch (start us, length us, event | category | flops | bytes accessed | tf_op | source)
XLA Modules:
  0.0 315.0 jit_solution(673930685689766179)
XLA Ops:
  0.6 0.7 and_select_fusion
  1.3 0.1 iota_add_fusion
  2.0 0.7 fusion
  2.7 13.4 %all-gather = s32[8,1,64]{2,1,0:T(1,128)S(1)} all-gather(s32[1,1,64]{2,1,0:T(1,128)S(1)} %fusion), channel_id=1, replica_groups=mesh['row'=4,'col'=8] {'col'}, dimensions={0}, use_global_device_ids=true | all-gather | bytes 2304 | tf_op jit(solution)/shard_map/all_gather | solution.py:490
  16.1 8.8 %select_reduce_fusion.2 = s32[64,8,16]{2,1,0:T(8,128)S(1)} fusion(s32[8,64]{1,0:T(8,128)S(1)} %multiply_add_fusion, s32[64,16]{1,0:T(8,128)S(1)} %iota_add_fusion, s32[8,64]{1,0:T(8,128)S(1)} %bitcast.54), kind=kLoop, calls=%fused_computation.4 | loop fusion | flops 1564672 | bytes 40960 | tf_op jit(solution)/shard_map/reduce_max | solution.py:459
  25.0 0.1 copy.23
  25.2 0.1 copy.26
  25.3 0.1 copy.27
  25.4 0.1 copy.28
  25.5 0.1 broadcast_add_fusion
  26.3 0.7 fusion.1
  27.0 8.1 %all-gather.1 = s32[4,1,64]{2,1,0:T(1,128)S(1)} all-gather(s32[1,1,64]{2,1,0:T(1,128)S(1)} %fusion.1), channel_id=1, replica_groups=mesh['row'=4,'col'=8] {'row'}, dimensions={0}, use_global_device_ids=true | all-gather | bytes 1280 | tf_op jit(solution)/shard_map/all_gather | solution.py:491
  35.1 9.2 %select_reduce_fusion.1 = s32[64,2,4,16]{3,2,1,0:T(4,128)S(1)} fusion(s32[4,64]{1,0:T(4,128)S(1)} %multiply_add_fusion.1, s32[64,2,16]{2,1,0:T(2,128)S(1)} %broadcast_add_fusion, s32[4,64]{1,0:T(4,128)S(1)} %bitcast.55), kind=kLoop, calls=%fused_computation.3 | loop fusion | flops 1564672 | bytes 43008 | tf_op jit(solution)/shard_map/reduce_max | solution.py:464
  44.3 0.1 copy.24
  44.4 0.1 copy.25
  45.2 0.1 add_select_fusion
  45.3 1.2 convert_reduce_fusion
  46.5 1.7 select_reduce_fusion.codes
  48.2 1.3 convert_reduce_fusion.1.counts
  49.5 0.0 copy-start.4
  49.5 0.7 copy-done.4
  50.1 93.3 %shard_map.95.p_own = bf16[64,128,128]{2,1,0:T(8,128)(2,1)S(1)} custom-call(s32[64]{0:T(128)S(1)} %bitcast.47, s32[1]{0:T(128)} %bitcast.40.count, bf16[32,128,2048]{2,1,0:T(8,128)(2,1)} %bitcast.48), custom_call_target="tpu_custom_call" | custom-call | tf_op jit(solution)/shard_map/pallas_call | solution.py:252
  143.5 0.0 copy-start
  143.5 1.3 copy-done
  144.8 0.0 copy-start.1
  144.8 152.0 %shard_map.96 = (bf16[8,64,128,128]{3,2,1,0:T(8,128)(2,1)}, bf16[4,64,128,128]{3,2,1,0:T(8,128)(2,1)}) custom-call(bf16[64,128,128]{2,1,0:T(8,128)(2,1)} %copy-done, bf16[64,128,128]{2,1,0:T(8,128)(2,1)} %bitcast.45), custom_call_target="tpu_custom_call" | custom-call | tf_op jit(solution)/shard_map/pallas_call | solution.py:380
  296.8 0.0 copy-done.1
  296.8 0.0 copy-start.2
  296.8 3.4 %copy-done.2 = bf16[4,64,128,128]{3,2,1,0:T(8,128)(2,1)S(1)} copy-done((bf16[4,64,128,128]{3,2,1,0:T(8,128)(2,1)S(1)}, bf16[4,64,128,128]{3,2,1,0:T(8,128)(2,1)}, u32[]{:S(2)}) %copy-start.2) | copy-done | bytes 8388632
  300.2 0.0 copy-start.3
  300.2 1.6 copy-done.3
  301.7 11.9 %shard_map.97 = f32[64,128,128]{2,1,0:T(8,128)} custom-call(s32[64,128]{1,0:T(8,128)S(1)} %select_reduce_fusion.codes, s32[64]{0:T(128)S(1)} %convert_reduce_fusion.1.counts, bf16[64,128,128]{2,1,0:T(8,128)(2,1)S(1)} %copy-done.1, bf16[64,128,128]{2,1,0:T(8,128)(2,1)S(1)} %bitcast.46, bf16[8,64,128,128]{3,2,1,0:T(8,128)(2,1)} %get-tuple-element.4.p_all, ...), custom_call_target="tpu_custom_call" | custom-call | tf_op jit(solution)/shard_map/pallas_call | solution.py:436
  313.6 1.3 copy.34
  (8 shorter events, 0.1 us)
Async XLA Ops:
  49.5 0.7 copy-start.4
  143.5 1.3 copy-start
  144.8 152.0 %copy-start.1 = (bf16[64,128,128]{2,1,0:T(8,128)(2,1)S(1)}, bf16[64,128,128]{2,1,0:T(8,128)(2,1)}, u32[]{:S(2)}) copy-start(bf16[64,128,128]{2,1,0:T(8,128)(2,1)} %copy-done) | copy-start | bytes 6291460
  296.8 3.4 %copy-start.2 = (bf16[4,64,128,128]{3,2,1,0:T(8,128)(2,1)S(1)}, bf16[4,64,128,128]{3,2,1,0:T(8,128)(2,1)}, u32[]{:S(2)}) copy-start(bf16[4,64,128,128]{3,2,1,0:T(8,128)(2,1)} %get-tuple-element.5.s_all) | copy-start | bytes 25165828
  300.2 1.6 copy-start.3

commit v2 on v1

--- a/solution.py
+++ b/solution.py
@@ -12,6 +12,10 @@
 CHUNK = 256
 PIECE = 2
 DEPTH = 3
+LANES = 128
+CODE = 512
+P_CAP = 44
+S_CAP = 32
 
 
 def rows_kernel(rows_n, cols_n, coeffs, out, send, recv):
@@ -135,13 +139,49 @@
     )(ids, count, coeffs, others)
 
 
-def panel_kernel(rows_n, cols_n, chunks, parts, depth, ids, count, coeffs, out, *scratch):
-    left, total, send, recv, sem = scratch[chunks:]
-    right = scratch[:chunks]
+def nt(x, y, precision=None):
+    return lax.dot_general(
+        x, y, (((1,), (1,)), ((), ())), precision=precision, preferred_element_type=jnp.float32
+    )
+
+
+def nn(x, y, precision=None):
+    return jnp.dot(x, y, precision=precision, preferred_element_type=jnp.float32)
+
+
+def iota(shape, dim):
+    return lax.broadcasted_iota(jnp.int32, shape, dim)
+
+
+def onehot(codes, height, kind=jnp.bfloat16):
+    hit = iota((height, LANES), 0) == codes
+    return jnp.where(hit, 1.0, 0.0).astype(kind)
+
+
+def flat(x):
+    return jnp.minimum(x, 1.0).astype(jnp.bfloat16)
+
+
+def panel_kernel(rows_n, cols_n, chunks, parts, depth, *refs):
+    ids, count, p_row, p_live, q_row, q_live, s_row, s_live, coeffs, s_in = refs[:10]
+    density, p_pair_out, p_recv, s_recv, codes, counts, flags_out, meta_out = refs[10:18]
+    right = refs[18 : 18 + chunks]
+    (
+        left, total, p_pair, s_own, p_pack, s_pack, meta, flags,
+        p_dense, q_dense, q_wide, s_dense, p_need, p_rank, s_need, s_rank, lists, lists_s,
+        send, recv, sem, meta_send, meta_recv, flag_send, flag_recv,
+        pair_send, pair_recv, p_send, p_got, pass_send, pass_recv, s_send, s_got, done,
+    ) = refs[18 + chunks :]
     row, col = lax.axis_index("row"), lax.axis_index("col")
+    slots = ids.shape[0]
     sub = cols_n // rows_n
+    zs = cols_n // 2
+    tile_rows = left.shape[0]
     tile_cols, _, wide = right[0].shape
+    bits = tile_cols.bit_length() - 1
     size = tile_cols // (2 * parts)
+    p_cap, s_cap = p_recv.shape[1] * p_recv.shape[2], s_recv.shape[1]
+    z, core = lax.div(col, 2), lax.rem(col, 2)
     owner = lax.div(col, sub)
     first = lax.rem(col, sub) * tile_cols
     y, x = lax.div(row, 2), lax.rem(row, 2)
@@ -155,6 +195,19 @@
         jnp.where(dx == dy, along_y, along_x),
     ]
     steps = [(k, part) for k in range(chunks) for part in range(parts)]
+    partner = {"row": row, "col": z * 2 + 1 - core}
+    row_mates = [{"row": row, "col": lax.rem(col + n, cols_n)} for n in range(1, cols_n)]
+    col_mates = [{"row": lax.rem(row + n, rows_n), "col": col} for n in range(1, rows_n)]
+
+    def remote(src, dst, send_sem, recv_sem, device):
+        return pltpu.make_async_remote_copy(
+            src_ref=src,
+            dst_ref=dst,
+            send_sem=send_sem,
+            recv_sem=recv_sem,
+            device_id=device,
+            device_id_type=MESH,
+        )
 
     def offset(way, part):
         return (way * parts + part) * size
@@ -168,14 +221,9 @@
 
     def copy(way, k, part):
         where = right[k].at[pl.ds(offset(way, part), size)]
-        return pltpu.make_async_remote_copy(
-            src_ref=where,
-            dst_ref=where,
-            send_sem=send.at[way, k * parts + part],
-            recv_sem=recv.at[way, k * parts + part],
-            device_id={"row": following[way], "col": col},
-            device_id_type=MESH,
-        )
+        device = {"row": following[way], "col": col}
+        at = k * parts + part
+        return remote(where, where, send.at[way, at], recv.at[way, at], device)
 
     @pl.when(is_source)
     def _():
@@ -184,14 +232,214 @@
                 load(way, k, part).start()
 
     load_left = pltpu.make_async_copy(coeffs, left, sem.at[0])
+    load_s = pltpu.make_async_copy(s_in, s_own, sem.at[1])
     load_left.start()
+    load_s.start()
+
+    mine = jnp.full((8, LANES), -1, jnp.int32)
+    lane = iota((8, LANES), 1)
+    height = iota((8, LANES), 0)
+    for at, (codes_in, live_in) in enumerate(((p_row, p_live), (q_row, q_live), (s_row, s_live))):
+        keep = jnp.logical_and(height == at, lane < live_in[0])
+        mine = jnp.where(keep, codes_in[...], mine)
+    meta[row, col] = mine
+
     barrier = pltpu.get_barrier_semaphore()
-    for near in (along_x, along_y):
-        pl.semaphore_signal(
-            barrier, inc=1, device_id={"row": near, "col": col}, device_id_type=MESH
-        )
-    pl.semaphore_wait(barrier, 2)
-    live = count[0]
+    for device in row_mates + col_mates:
+        pl.semaphore_signal(barrier, inc=1, device_id=device, device_id_type=MESH)
+    pl.semaphore_wait(barrier, len(row_mates) + len(col_mates))
+
+    def along_row(table, send_sem, recv_sem, source, n):
+        where = table.at[row, source]
+        return remote(where, where, send_sem.at[n], recv_sem.at[source], row_mates[n])
+
+    def along_col(table, send_sem, recv_sem, source, n):
+        where = table.at[source]
+        at = len(row_mates) + n
+        return remote(where, where, send_sem.at[at], recv_sem.at[cols_n + source], col_mates[n])
+
+    def spread(table, send_sem, recv_sem):
+        def first_half():
+            for n in range(cols_n - 1):
+                along_row(table, send_sem, recv_sem, col, n).start()
+
+        def second_half():
+            for n in range(cols_n - 1):
+                source = lax.rem(col + cols_n - 1 - n, cols_n)
+                along_row(table, send_sem, recv_sem, source, n).wait_recv()
+            for n in range(rows_n - 1):
+                along_col(table, send_sem, recv_sem, row, n).start()
+
+        def last():
+            for n in range(rows_n - 1):
+                source = lax.rem(row + rows_n - 1 - n, rows_n)
+                along_col(table, send_sem, recv_sem, source, n).wait_recv()
+            for n in range(cols_n - 1):
+                along_row(table, send_sem, recv_sem, col, n).wait_send()
+            for n in range(rows_n - 1):
+                along_col(table, send_sem, recv_sem, row, n).wait_send()
+
+        return first_half, second_half, last
+
+    meta_steps = spread(meta, meta_send, meta_recv)
+    flag_steps = spread(flags, flag_send, flag_recv)
+    meta_steps[0]()
+
+    def code(at, r, c):
+        return meta[r, c][at : at + 1]
+
+    def split(at, r, c):
+        value = code(at, r, c)
+        return value >> bits, c * tile_cols + (value & (tile_cols - 1))
+
+    def split_s(r, c):
+        value = code(2, r, c)
+        local = value >> bits
+        k = (r + rows_n * (local >> bits)) * tile_cols + (local & (tile_cols - 1))
+        return k, c * tile_cols + (value & (tile_cols - 1))
+
+    lanes = iota((1, LANES), 1)
+    ahead = jnp.where(iota((LANES, LANES), 0) <= iota((LANES, LANES), 1), 1.0, 0.0)
+    ahead = ahead.astype(jnp.bfloat16)
+    exact = lax.Precision.HIGHEST
+
+    def dense_rows(r):
+        p_sum = jnp.zeros((LANES, tile_rows), jnp.float32)
+        q_sum = jnp.zeros((LANES, tile_rows), jnp.float32)
+        q_turn = jnp.zeros((tile_rows, LANES), jnp.float32)
+        for c in range(cols_n):
+            a, k = split(0, r, c)
+            p_sum += nt(onehot(k, LANES), onehot(a, tile_rows))
+            a, k = split(1, r, c)
+            at_row, at_col = onehot(a, tile_rows), onehot(k, LANES)
+            q_sum += nt(at_col, at_row)
+            q_turn += nt(at_row, at_col)
+        p_dense[r] = p_sum.astype(jnp.bfloat16)
+        q_dense[r] = q_sum.astype(jnp.bfloat16)
+        q_wide[r] = q_turn.astype(jnp.bfloat16)
+
+    def dense_s():
+        s_sum = jnp.zeros((LANES, LANES), jnp.float32)
+        for r in range(rows_n):
+            for c in range(cols_n):
+                k, j = split_s(r, c)
+                s_sum += nt(onehot(k, LANES), onehot(j, LANES))
+        s_dense[...] = s_sum.astype(jnp.bfloat16)
+
+    def need_p():
+        wants = []
+        for d in range(zs):
+            group = lax.broadcasted_iota(jnp.int32, (tile_rows, LANES), 1) // (2 * tile_cols)
+            part = jnp.where(group == d, q_wide[row].astype(jnp.float32), 0.0)
+            wants.append(flat(nt(s_dense[...], part.astype(jnp.bfloat16))))
+        for c in range(cols_n):
+            a, k = split(0, row, c)
+            at_row, at_k = onehot(a, tile_rows), onehot(k, LANES, jnp.float32)
+            for d in range(zs):
+                hit = jnp.sum(nn(wants[d], at_row) * at_k, axis=0, keepdims=True)
+                p_need[pl.ds(d * cols_n + c, 1)] = jnp.minimum(hit, 1.0)
+        rank = nn(p_need[: zs * cols_n].astype(jnp.bfloat16), ahead)
+        before = pltpu.roll(jnp.max(rank, axis=1, keepdims=True) + jnp.zeros_like(rank), 1, 0)
+        odd = iota(rank.shape, 0) % 2 == 1
+        p_rank[: zs * cols_n] = rank + jnp.where(odd, before, 0.0)
+
+    def need_s():
+        for r in range(rows_n):
+            wants = flat(nt(q_dense[r], p_dense[r]))
+            for source in range(rows_n):
+                k, j = split_s(source, col)
+                hit = nn(wants, onehot(k, LANES)) * onehot(j, LANES, jnp.float32)
+                hit = jnp.sum(hit, axis=0, keepdims=True)
+                s_need[pl.ds(r * rows_n + source, 1)] = jnp.minimum(hit, 1.0)
+        square = rows_n * rows_n
+        s_rank[:square] = nn(s_need[:square].astype(jnp.bfloat16), ahead)
+
+    def picks(need, rank, base):
+        chosen = jnp.logical_and(rank == (iota((LANES, LANES), 0) + 1).astype(jnp.float32), need > 0)
+        chosen = jnp.where(chosen, 1.0, 0.0).astype(jnp.bfloat16)
+        values = (base + lane).astype(jnp.float32).astype(jnp.bfloat16)
+        return nt(values, chosen)
+
+    def make_lists():
+        made = jnp.zeros((8, LANES), jnp.float32)
+        for d in range(zs):
+            entry = jnp.zeros((8, LANES), jnp.float32)
+            for half in range(2):
+                at = d * cols_n + z * 2 + half
+                entry += picks(p_need[pl.ds(at, 1)], p_rank[pl.ds(at, 1)], half * slots)
+            made = jnp.where(height == d, entry, made)
+        for r in range(rows_n):
+            at = r * rows_n + row
+            entry = picks(s_need[pl.ds(at, 1)], s_rank[pl.ds(at, 1)], 0)
+            made = jnp.where(height == zs + r, entry, made)
+        lists[...] = made.astype(jnp.int32)
+        over = jnp.zeros((1, 1), jnp.float32)
+        for d in range(zs):
+            most = jnp.max(p_rank[pl.ds(z * cols_n + d * 2 + 1, 1)], axis=1, keepdims=True)
+            over = jnp.maximum(over, jnp.where(d == z, 0.0, most - p_cap))
+        for r in range(rows_n):
+            most = jnp.max(s_rank[pl.ds(row * rows_n + r, 1)], axis=1, keepdims=True)
+            over = jnp.maximum(over, jnp.where(r == row, 0.0, most - s_cap))
+        flags[row, col] = (over + jnp.zeros((8, LANES), jnp.float32)).astype(jnp.int32)
+
+    def make_codes():
+        p_at = jnp.zeros((tile_rows, LANES), jnp.float32)
+        for c in range(cols_n):
+            a, k = split(0, row, c)
+            at = z * cols_n + c
+            own = (c % 2 * slots + 1 + lanes).astype(jnp.float32)
+            far = 2 * slots + c // 2 * p_cap + p_rank[pl.ds(at, 1)]
+            far = jnp.where(p_need[pl.ds(at, 1)] > 0, far, 0.0)
+            place = jnp.where(c // 2 == z, own, far)
+            p_at += nt(
+                onehot(a, tile_rows, jnp.float32) * place, onehot(k, LANES, jnp.float32), exact
+            )
+        s_at = jnp.zeros((LANES, LANES), jnp.float32)
+        for r in range(rows_n):
+            k, j = split_s(r, col)
+            at = row * rows_n + r
+            own = (1 + lanes).astype(jnp.float32)
+            far = slots + r * s_cap + s_rank[pl.ds(at, 1)]
+            far = jnp.where(s_need[pl.ds(at, 1)] > 0, far, 0.0)
+            place = jnp.where(r == row, own, far)
+            s_at += nt(onehot(j, LANES, jnp.float32) * place, onehot(k, LANES, jnp.float32), exact)
+        a, j = split(1, row, col)
+        unit = onehot(lanes, LANES)
+        q_row_hot = nt(unit, onehot(a, tile_rows))[:slots]
+        q_col_hot = nt(unit, onehot(j, LANES))[:slots]
+        p_for = nn(q_row_hot, p_at, exact)
+        s_for = nn(q_col_hot, s_at, exact)
+        match = jnp.where(jnp.logical_and(p_for > 0, s_for > 0), 1.0, 0.0)
+        value = (p_for - 1) * CODE + (s_for - 1)
+        rank = nn(match.astype(jnp.bfloat16), ahead) * match
+        counts[...] = nt(
+            jnp.ones((8, LANES), jnp.bfloat16), match.astype(jnp.bfloat16)
+        ).astype(jnp.int32)
+
+        def place_one(n, made):
+            here = jnp.where(rank == (n + 1).astype(jnp.float32), value, 0.0)
+            here = jnp.sum(here, axis=1, keepdims=True)
+            return jnp.where(iota(made.shape, 1) == n, here, made)
+
+        made = lax.fori_loop(0, LANES, place_one, jnp.zeros((slots, LANES), jnp.float32))
+        codes[...] = made.astype(jnp.int32)
+
+    load_lists = pltpu.make_async_copy(lists, lists_s, sem.at[2])
+
+    def before_three():
+        make_lists()
+        flag_steps[0]()
+        load_lists.start()
+
+    work = {
+        0: [meta_steps[1], meta_steps[2]],
+        1: [lambda: dense_rows(0), lambda: dense_rows(1)],
+        2: [lambda: dense_rows(2), lambda: dense_rows(3), dense_s],
+        3: [need_p],
+        4: [need_s, before_three],
+        5: [flag_steps[1], make_codes],
+        6: [flag_steps[2]],
+    }
 
     def relay(k):
         for part in range(parts):
@@ -205,6 +453,17 @@
                         copy(way, *steps[now - depth]).wait_send()
                     copy(way, k, part).start()
 
+    groups = 4
+    group = slots // groups
+
+    def pair_copy(n):
+        where = p_pair.at[pl.ds(core * slots + n * group, group)]
+        return remote(where, where, pair_send.at[n], pair_recv.at[n], partner)
+
+    def pair_got(n):
+        where = p_pair.at[pl.ds((1 - core) * slots + n * group, group)]
+        return remote(where, where, pair_send.at[n], pair_recv.at[n], partner)
+
     relay(0)
     load_left.wait()
     for k in range(chunks):
@@ -219,8 +478,8 @@
 
         def block(slot, carry, k=k):
             raw = lax.dot_general(
-                left[lax.div(ids[slot], tile_cols), :, pl.ds(k * wide, wide)],
-                right[k][lax.rem(ids[slot], tile_cols)],
+                left[ids[slot] >> bits, :, pl.ds(k * wide, wide)],
+                right[k][ids[slot] & (tile_cols - 1)],
                 (((1,), (1,)), ((), ())),
                 preferred_element_type=jnp.float32,
             )
@@ -229,11 +488,76 @@
             if k < chunks - 1:
                 total[slot] = raw
             else:
-                out[slot] = jnp.where(slot < live, raw, 0.0).astype(out.dtype)
+                raw = jnp.where(slot < count[0], raw, 0.0)
+                p_pair[core * slots + slot] = raw.astype(p_pair.dtype)
             return carry
 
-        lax.fori_loop(0, out.shape[0], block, 0, unroll=4)
-
+        if k < chunks - 1:
+            lax.fori_loop(0, slots, block, 0, unroll=4)
+            for one in work.get(k, []):
+                one()
+        else:
+            for n in range(groups):
+                lax.fori_loop(n * group, (n + 1) * group, block, 0, unroll=4)
+                pair_copy(n).start()
+
+    density_out = pltpu.make_async_copy(p_pair.at[pl.ds(core * slots, slots)], density, done.at[0])
+    density_out.start()
+    load_s.wait()
+    load_lists.wait()
+
+    def s_copy(n):
+        r = col_mates[n]["row"]
+        return remote(s_pack.at[n], s_recv.at[row], s_send.at[n], s_got.at[row], col_mates[n])
+
+    def s_arrival(n):
+        source = col_mates[n]["row"]
+        return remote(s_pack.at[n], s_recv.at[source], s_send.at[n], s_got.at[source], col_mates[n])
+
+    for n in range(groups):
+        pair_got(n).wait_recv()
+    pair_out = pltpu.make_async_copy(p_pair, p_pair_out, done.at[1])
+    pair_out.start()
+
+    def chip(n):
+        return lax.rem(z + n + 1, zs)
+
+    def p_copy(n):
+        device = {"row": row, "col": chip(n) * 2 + core}
+        return remote(p_pack.at[n], p_recv.at[z, core], p_send.at[n], p_got.at[z], device)
+
+    def p_arrival(n):
+        where = p_recv.at[chip(n), core]
+        return remote(p_pack.at[n], where, p_send.at[n], p_got.at[chip(n)], partner)
+
+    def p_pass(n, half):
+        where = p_recv.at[chip(n), half]
+        return remote(where, where, pass_send.at[n], pass_recv.at[chip(n)], partner)
+
+    for n in range(zs - 1):
+        start = core * (p_cap // 2)
+
+        def fill(t, carry, n=n):
+            at = lists_s[chip(n), core * (p_cap // 2) + t]
+            p_pack[n, t] = p_pair[jnp.clip(at, 0, 2 * slots - 1)]
+            return carry
+
+        lax.fori_loop(0, p_cap // 2, fill, 0, unroll=2)
+        p_copy(n).start()
+    for n in range(rows_n - 1):
+
+        def fill_s(t, carry, n=n):
+            at = lists_s[zs + col_mates[n]["row"], t]
+            s_pack[n, t] = s_own[jnp.clip(at, 0, s_own.shape[0] - 1)]
+            return carry
+
+        lax.fori_loop(0, s_cap, fill_s, 0, unroll=2)
+        s_copy(n).start()
+
+    flags_go = pltpu.make_async_copy(flags, flags_out, done.at[2])
+    meta_go = pltpu.make_async_copy(meta, meta_out, done.at[3])
+    flags_go.start()
+    meta_go.start()
     for way in range(2):
 
         @pl.when(sends[way])
@@ -241,32 +565,147 @@
             for k, part in steps[-depth:]:
                 copy(way, k, part).wait_send()
 
-
-def panel_density(ids, count, coeffs, rows_n, cols_n):
-    slots = ids.shape[0]
+    for n in range(groups):
+        pair_copy(n).wait_send()
+    for n in range(zs - 1):
+        p_arrival(n).wait_recv()
+        p_pass(n, core).start()
+    for n in range(rows_n - 1):
+        s_arrival(n).wait_recv()
+        s_copy(n).wait_send()
+    for n in range(zs - 1):
+        p_pass(n, 1 - core).wait_recv()
+        p_pass(n, core).wait_send()
+        p_copy(n).wait_send()
+    density_out.wait()
+    pair_out.wait()
+    flags_go.wait()
+    meta_go.wait()
+
+
+def panel_density(ids, counts, coeffs, s_own, rows_n, cols_n):
+    slots = ids[0].shape[0]
     orbitals = coeffs.shape[1]
     blocks = coeffs.reshape(-1, 128, orbitals)
-    tile_cols = blocks.shape[0] * rows_n // cols_n
+    tile_rows = blocks.shape[0]
+    tile_cols = tile_rows * rows_n // cols_n
     chunks = max(1, orbitals // CHUNK)
     parts = max(1, tile_cols // (2 * PIECE))
+    zs = cols_n // 2
+    half = P_CAP // 2
+    kind = coeffs.dtype
+    block = (128, 128)
+    smem, vmem = pl.BlockSpec(memory_space=pltpu.SMEM), pl.BlockSpec(memory_space=pltpu.VMEM)
+    anywhere = pl.BlockSpec(memory_space=pl.ANY)
+    rows = [jnp.pad(one[None], ((0, 0), (0, LANES - slots)), constant_values=-1) for one in ids]
+    table = (rows_n, cols_n, 8, LANES)
+    sems = pltpu.SemaphoreType.DMA
+    floats = [
+        pltpu.VMEM((rows_n, LANES, tile_rows), jnp.bfloat16),
+        pltpu.VMEM((rows_n, LANES, tile_rows), jnp.bfloat16),
+        pltpu.VMEM((rows_n, tile_rows, LANES), jnp.bfloat16),
+        pltpu.VMEM((LANES, LANES), jnp.bfloat16),
+        pltpu.VMEM((zs * cols_n + 8, LANES), jnp.float32),
+        pltpu.VMEM((zs * cols_n + 8, LANES), jnp.float32),
+        pltpu.VMEM((rows_n * rows_n + 8, LANES), jnp.float32),
+        pltpu.VMEM((rows_n * rows_n + 8, LANES), jnp.float32),
+    ]
     return pl.pallas_call(
         functools.partial(panel_kernel, rows_n, cols_n, chunks, parts, DEPTH),
-        out_shape=jax.ShapeDtypeStruct((slots, 128, 128), jnp.bfloat16),
-        in_specs=[pl.BlockSpec(memory_space=pltpu.SMEM)] * 2
-        + [pl.BlockSpec(memory_space=pl.ANY)],
-        out_specs=pl.BlockSpec(memory_space=pltpu.VMEM),
-        scratch_shapes=[pltpu.VMEM((tile_cols, 128, orbitals // chunks), coeffs.dtype)] * chunks
+        out_shape=(
+            jax.ShapeDtypeStruct((slots,) + block, kind),
+            jax.ShapeDtypeStruct((2 * slots,) + block, kind),
+            jax.ShapeDtypeStruct((zs, 2, half) + block, kind),
+            jax.ShapeDtypeStruct((rows_n, S_CAP) + block, kind),
+            jax.ShapeDtypeStruct((slots, LANES), jnp.int32),
+            jax.ShapeDtypeStruct((8, slots), jnp.int32),
+            jax.ShapeDtypeStruct(table, jnp.int32),
+            jax.ShapeDtypeStruct(table, jnp.int32),
+        ),
+        in_specs=[smem, smem] + [vmem, smem] * 3 + [anywhere] * 2,
+        out_specs=[anywhere] * 4 + [vmem] * 2 + [anywhere] * 2,
+        scratch_shapes=[pltpu.VMEM((tile_cols, 128, orbitals // chunks), kind)] * chunks
         + [
-            pltpu.VMEM(blocks.shape, coeffs.dtype),
-            pltpu.VMEM((slots, 128, 128), jnp.float32),
-            pltpu.SemaphoreType.DMA((2, chunks * parts)),
-            pltpu.SemaphoreType.DMA((2, chunks * parts)),
-            pltpu.SemaphoreType.DMA((1,)),
+            pltpu.VMEM(blocks.shape, kind),
+            pltpu.VMEM((slots,) + block, jnp.float32),
+            pltpu.VMEM((2 * slots,) + block, kind),
+            pltpu.VMEM((slots,) + block, kind),
+            pltpu.VMEM((zs - 1, half) + block, kind),
+            pltpu.VMEM((rows_n - 1, S_CAP) + block, kind),
+            pltpu.VMEM(table, jnp.int32),
+            pltpu.VMEM(table, jnp.int32),
+        ]
+        + floats
+        + [
+            pltpu.VMEM((8, LANES), jnp.int32),
+            pltpu.SMEM((8, LANES), jnp.int32),
+            sems((2, chunks * parts)),
+            sems((2, chunks * parts)),
+            sems((3,)),
+            sems((cols_n + rows_n - 2,)),
+            sems((cols_n + rows_n,)),
+            sems((cols_n + rows_n - 2,)),
+            sems((cols_n + rows_n,)),
+            sems((4,)),
+            sems((4,)),
+            sems((zs - 1,)),
+            sems((zs,)),
+            sems((zs - 1,)),
+            sems((zs,)),
+            sems((rows_n - 1,)),
+            sems((rows_n,)),
+            sems((4,)),
         ],
         compiler_params=pltpu.CompilerParams(
-            collective_id=2, has_side_effects=True, vmem_limit_bytes=40 * MIB
+            collective_id=2, has_side_effects=True, vmem_limit_bytes=60 * MIB
         ),
-    )(ids, count, blocks)
+    )(ids[0], counts[0], rows[0], counts[0], rows[1], counts[1], rows[2], counts[2], blocks, s_own)
+
+
+def packed_kernel(codes, counts, p_pair, p_recv, s_own, s_recv, out, left, right, sem):
+    near, s_near = p_pair.shape[0], s_own.shape[0]
+    loads = [
+        pltpu.make_async_copy(p_pair, left.at[pl.ds(0, near)], sem.at[0]),
+        pltpu.make_async_copy(p_recv, left.at[pl.ds(near, p_recv.shape[0])], sem.at[1]),
+        pltpu.make_async_copy(s_own, right.at[pl.ds(0, s_near)], sem.at[2]),
+        pltpu.make_async_copy(s_recv, right.at[pl.ds(s_near, s_recv.shape[0])], sem.at[3]),
+    ]
+    for load in loads:
+        load.start()
+    for load in loads:
+        load.wait()
+
+    def slot(q, carry):
+        def term(n, total):
+            code = codes[q, n]
+            return total + jnp.dot(
+                left[lax.div(code, CODE)],
+                right[lax.rem(code, CODE)],
+                preferred_element_type=jnp.float32,
+            )
+
+        out[q] = lax.fori_loop(0, counts[0, q], term, jnp.zeros((128, 128), jnp.float32))
+        return carry
+
+    lax.fori_loop(0, out.shape[0], slot, 0)
+
+
+def packed_product(codes, counts, p_pair, p_recv, s_own, s_recv):
+    p_recv = p_recv.reshape(-1, 128, 128)
+    s_recv = s_recv.reshape(-1, 128, 128)
+    return pl.pallas_call(
+        packed_kernel,
+        out_shape=jax.ShapeDtypeStruct((codes.shape[0], 128, 128), jnp.float32),
+        in_specs=[pl.BlockSpec(memory_space=pltpu.SMEM)] * 2
+        + [pl.BlockSpec(memory_space=pl.ANY)] * 4,
+        out_specs=pl.BlockSpec(memory_space=pltpu.VMEM),
+        scratch_shapes=[
+            pltpu.VMEM((p_pair.shape[0] + p_recv.shape[0], 128, 128), p_pair.dtype),
+            pltpu.VMEM((s_own.shape[0] + s_recv.shape[0], 128, 128), s_own.dtype),
+            pltpu.SemaphoreType.DMA((4,)),
+        ],
+        compiler_params=pltpu.CompilerParams(vmem_limit_bytes=40 * MIB),
+    )(codes, counts, p_pair, p_recv, s_own, s_recv)
 
 
 def blocks_kernel(rows_n, cols_n, parts, p_own, s_own, p_all, s_all, *sems):
@@ -487,18 +926,35 @@
     def live(ids, count):
         return jnp.arange(ids.shape[0], dtype=jnp.int32) < count[0, 0]
 
-    p_codes = lax.all_gather(jnp.where(live(p_ids, p_count), p_ids, -1), "col")
-    s_codes = lax.all_gather(jnp.where(live(s_ids, s_count), s_ids, -1), "row")
-    codes, counts = match_lists(
-        p_codes, s_codes, q_ids, live(q_ids, q_count), tile_cols, cols_n // rows_n
-    )
-    if rows_n == 4:
-        p_own = panel_density(p_ids, p_count[0], coeffs, rows_n, cols_n)
+    def whole(p_codes, s_codes, p_own):
+        codes, counts = match_lists(
+            p_codes, s_codes, q_ids, live(q_ids, q_count), tile_cols, cols_n // rows_n
+        )
+        p_all, s_all = gather_blocks(p_own, s_own, rows_n, cols_n)
+        return block_product(codes, counts, p_own, s_own, p_all, s_all)
+
+    if rows_n == 4 and tile_cols * cols_n == LANES and max(p_max, s_max, q_max) <= LANES // 2:
+        counts = (p_count[0], q_count[0], s_count[0])
+        p_own, p_pair, p_recv, s_recv, codes, pairs, over, meta = panel_density(
+            (p_ids, q_ids, s_ids), counts, coeffs, s_own, rows_n, cols_n
+        )
+
+        def full():
+            row, col = lax.axis_index("row"), lax.axis_index("col")
+            p_codes = lax.dynamic_index_in_dim(meta, row, 0, False)[:, 0, :p_max]
+            s_codes = lax.dynamic_index_in_dim(meta, col, 1, False)[:, 2, :s_max]
+            return whole(p_codes, s_codes, p_own)
+
+        def packed():
+            return packed_product(codes, pairs, p_pair, p_recv, s_own, s_recv)
+
+        product = lax.cond(jnp.max(over) > 0, full, packed)
     else:
+        p_codes = lax.all_gather(jnp.where(live(p_ids, p_count), p_ids, -1), "col")
+        s_codes = lax.all_gather(jnp.where(live(s_ids, s_count), s_ids, -1), "row")
         others = gather_rows(coeffs, rows_n, cols_n)
         p_own = density(p_ids, p_count[0], coeffs, others, rows_n, cols_n)
-    p_all, s_all = gather_blocks(p_own, s_own, rows_n, cols_n)
-    product = block_product(codes, counts, p_own, s_own, p_all, s_all)
+        product = whole(p_codes, s_codes, p_own)
     return (p_own.reshape(1, 1, p_max, 128, 128), product.reshape(1, 1, q_max, 128, 128))
 
 

time: 317 us -> 251 us (0.79)
  the two profiles are of different devices: /device:TPU:0 before, /device:TPU:31 now
where the time goes in v2:
time: 251 us; the launch traced here: 250 us
  Pallas kernels  238 us (95%)
  local copies, waits for them, and re-layouts  6.72 us (3%)
  between operations  3.26 us (1%)
    pallas_call x1, Pallas kernels, panel_density(): pl.pallas_call(functools.partial(panel_kernel, rows_n, cols_n, chunks, pa...  226 us
    pallas_call x1, Pallas kernels, packed_product(): pl.pallas_call(packed_kernel, out_shape=jax.ShapeDtypeStruct((codes.shape...  12 us

profile of v2, /device:TPU:31, one launch (start us, length us, event | category | flops | bytes accessed | tf_op | source)
XLA Modules:
  0.0 249.7 jit_solution(17966459168283648090)
XLA Ops:
  2.6 1.2 pad.12.refs_6_
  3.8 1.2 pad.11.refs_4_
  5.0 1.2 pad.10.refs_2_
  6.1 0.0 copy-start.1
  6.1 0.0 copy-start.2
  6.1 225.9 %shard_map.95 = (bf16[64,128,128]{2,1,0:T(8,128)(2,1)}, bf16[128,128,128]{2,1,0:T(8,128)(2,1)}, bf16[4,2,22,128,128]{4,3,2,1,0:T(8,128)(2,1)}, bf16[4,32,128,128...) custom-call(s32[64]{0:T(128)} %bitcast.62, ...), custom_call_target="tpu_custom_call" | custom-call | tf_op jit(solution)/shard_map/pallas_call | solution.py:613
  232.0 1.6 reduce_max.27
  234.2 0.0 copy-done.1
  234.2 0.0 copy-done.2
  234.3 12.2 %conditional.1 = (f32[1,1,64,128,128]{4,3,2,1,0:T(8,128)}) conditional(s32[]{:T(128)} %convert_element_type.13, (bf16[4,2,22,128,128]{4,3,2,1,0:T(8,128)(2,1)}, bf16[4,32,128,128]{3,2,1,0:T(8,128)(2,1)}, s32[64,128]{1,0:T(8,128)S(1)}, s32[8,64]{1,0:T(8,128)S(1)}, bf16[128,128,128]{2,1,0:T(8,128)(2,1)}, ...), branch_computations={%region_1.2_spmd, %region_2.8_spmd} | conditional | flops 9533291 | bytes 34825320 | solution.py:951
  234.3 12.0 %branch_0_fun.1 = f32[64,128,128]{2,1,0:T(8,128)} custom-call(s32[64,128]{1,0:T(8,128)S(1)} %get-tuple-element.27.codes, s32[8,64]{1,0:T(8,128)S(1)} %get-tuple-element.28.counts, bf16[128,128,128]{2,1,0:T(8,128)(2,1)} %get-tuple-element.29.p_pair, bf16[176,128,128]{2,1,0:T(8,128)(2,1)} %bitcast.51, bf16[64,128,128]{2,1,0:T(8,128)(2,1)S(1)} %get-tuple-element.31.s_own, ...), custom_call_target="tpu_custom_call" | custom-call | tf_op jit(solution)/shard_map/cond/branch_0_fun/pallas_call | solution.py:696
  246.5 3.2 %copy.35 = bf16[1,1,64,128,128]{4,3,2,1,0:T(8,128)(2,1)} copy(bf16[1,1,64,128,128]{4,3,2,1,0:T(8,128)(2,1)} %bitcast.49) | data formatting | bytes 4194304
Async XLA Ops:
  6.1 228.1 %copy-start.1 = (bf16[1,1,64,128,128]{4,3,2,1,0:T(8,128)(2,1)S(1)}, bf16[1,1,64,128,128]{4,3,2,1,0:T(8,128)(2,1)}, u32[]{:S(2)}) copy-start(bf16[1,1,64,128,128]{4,3,2,1,0:T(8,128)(2,1)} %param.13) | copy-start | bytes 6291460
  6.1 228.1 %copy-start.2 = (s32[1,1,64]{2,1,0:T(1,128)S(1)}, s32[1,1,64]{2,1,0:T(1,128)}, u32[]{:S(2)}) copy-start(s32[1,1,64]{2,1,0:T(1,128)} %param.16) | copy-start | bytes 772

commit v3 on v2

--- a/solution.py
+++ b/solution.py
@@ -9,13 +9,13 @@
 
 MESH = pl.DeviceIdType.MESH
 MIB = 1 << 20
-CHUNK = 256
-PIECE = 2
 DEPTH = 3
+BATCH = 8
 LANES = 128
 CODE = 512
-P_CAP = 44
-S_CAP = 32
+PHASES = ((10, 4, 5, 30), (6, 4, 3, 20))
+LAG = 2
+S_CAP = 44
 
 
 def rows_kernel(rows_n, cols_n, coeffs, out, send, recv):
@@ -162,25 +162,35 @@
     return jnp.minimum(x, 1.0).astype(jnp.bfloat16)
 
 
-def panel_kernel(rows_n, cols_n, chunks, parts, depth, *refs):
+def panel_kernel(rows_n, cols_n, phases, depth, *refs):
+    stages = len(phases)
     ids, count, p_row, p_live, q_row, q_live, s_row, s_live, coeffs, s_in = refs[:10]
-    density, p_pair_out, p_recv, s_recv, codes, counts, flags_out, meta_out = refs[10:18]
-    right = refs[18 : 18 + chunks]
+    density, p_pair_out, s_recv, codes, counts, flags_out, meta_out = refs[10:17]
+    p_recv = refs[17 : 17 + stages]
+    refs = refs[17 + stages :]
+    right = []
+    for _, chunks, _, _ in phases:
+        right.append(refs[:chunks])
+        refs = refs[chunks:]
+    p_pair, p_pack = refs[:stages], refs[stages : 2 * stages]
     (
-        left, total, p_pair, s_own, p_pack, s_pack, meta, flags,
+        left, total, s_pair, s_pack, meta, flags,
         p_dense, q_dense, q_wide, s_dense, p_need, p_rank, s_need, s_rank, lists, lists_s,
         send, recv, sem, meta_send, meta_recv, flag_send, flag_recv,
-        pair_send, pair_recv, p_send, p_got, pass_send, pass_recv, s_send, s_got, done,
-    ) = refs[18 + chunks :]
+        pair_send, pair_recv, p_send, p_got, pass_send, pass_recv,
+        s_send, s_got, s_pass_send, s_pass_recv, s_swap, done,
+    ) = refs[2 * stages :]
     row, col = lax.axis_index("row"), lax.axis_index("col")
     slots = ids.shape[0]
     sub = cols_n // rows_n
     zs = cols_n // 2
     tile_rows = left.shape[0]
-    tile_cols, _, wide = right[0].shape
+    tile_cols = sum(phase[0] for phase in phases)
     bits = tile_cols.bit_length() - 1
-    size = tile_cols // (2 * parts)
-    p_cap, s_cap = p_recv.shape[1] * p_recv.shape[2], s_recv.shape[1]
+    caps = [phase[3] for phase in phases]
+    starts = [sum(phase[0] for phase in phases[:f]) for f in range(stages)]
+    bases = [2 * slots + zs * sum(caps[:f]) for f in range(stages)]
+    s_cap = s_recv.shape[1] * s_recv.shape[2]
     z, core = lax.div(col, 2), lax.rem(col, 2)
     owner = lax.div(col, sub)
     first = lax.rem(col, sub) * tile_cols
@@ -194,7 +204,8 @@
         jnp.where(dx == dy, along_x, along_y),
         jnp.where(dx == dy, along_y, along_x),
     ]
-    steps = [(k, part) for k in range(chunks) for part in range(parts)]
+    pieces = [(f, k) for f in range(stages) for k in range(phases[f][1])]
+    steps = [(f, k, part) for f, k in pieces for part in range(phases[f][2])]
     partner = {"row": row, "col": z * 2 + 1 - core}
     row_mates = [{"row": row, "col": lax.rem(col + n, cols_n)} for n in range(1, cols_n)]
     col_mates = [{"row": lax.rem(row + n, rows_n), "col": col} for n in range(1, rows_n)]
@@ -209,30 +220,33 @@
             device_id_type=MESH,
         )
 
-    def offset(way, part):
-        return (way * parts + part) * size
-
-    def load(way, k, part):
+    def area(way, f, part):
+        size = phases[f][0] // (2 * phases[f][2])
+        return (way * phases[f][2] + part) * size, size
+
+    def load(way, f, k, part):
+        at, size = area(way, f, part)
+        wide = right[f][k].shape[2]
         return pltpu.make_async_copy(
-            coeffs.at[pl.ds(first + offset(way, part), size), :, pl.ds(k * wide, wide)],
-            right[k].at[pl.ds(offset(way, part), size)],
-            recv.at[way, k * parts + part],
+            coeffs.at[pl.ds(first + starts[f] + at, size), :, pl.ds(k * wide, wide)],
+            right[f][k].at[pl.ds(at, size)],
+            recv.at[way, steps.index((f, k, part))],
         )
 
-    def copy(way, k, part):
-        where = right[k].at[pl.ds(offset(way, part), size)]
+    def copy(way, f, k, part):
+        where = right[f][k].at[pl.ds(*area(way, f, part))]
         device = {"row": following[way], "col": col}
-        at = k * parts + part
+        at = steps.index((f, k, part))
         return remote(where, where, send.at[way, at], recv.at[way, at], device)
 
     @pl.when(is_source)
     def _():
-        for k, part in steps:
+        for step in steps:
             for way in range(2):
-                load(way, k, part).start()
+                load(way, *step).start()
 
     load_left = pltpu.make_async_copy(coeffs, left, sem.at[0])
-    load_s = pltpu.make_async_copy(s_in, s_own, sem.at[1])
+    load_s = pltpu.make_async_copy(s_in, s_pair.at[pl.ds(core * slots, slots)], sem.at[1])
     load_left.start()
     load_s.start()
 
@@ -326,6 +340,18 @@
                 s_sum += nt(onehot(k, LANES), onehot(j, LANES))
         s_dense[...] = s_sum.astype(jnp.bfloat16)
 
+    def ranked(need, rank, size):
+        plain = nn(need[:size].astype(jnp.bfloat16), ahead)
+        before = pltpu.roll(jnp.max(plain, axis=1, keepdims=True) + jnp.zeros_like(plain), 1, 0)
+        odd = iota(plain.shape, 0) % 2 == 1
+        rank[:size] = plain + jnp.where(odd, before, 0.0)
+
+    def p_at(f, d, c):
+        return (f * zs + d) * cols_n + c
+
+    def s_at(r, source, half):
+        return (r * rows_n + source) * 2 + half
+
     def need_p():
         wants = []
         for d in range(zs):
@@ -335,24 +361,25 @@
         for c in range(cols_n):
             a, k = split(0, row, c)
             at_row, at_k = onehot(a, tile_rows), onehot(k, LANES, jnp.float32)
+            b = k - c * tile_cols
             for d in range(zs):
                 hit = jnp.sum(nn(wants[d], at_row) * at_k, axis=0, keepdims=True)
-                p_need[pl.ds(d * cols_n + c, 1)] = jnp.minimum(hit, 1.0)
-        rank = nn(p_need[: zs * cols_n].astype(jnp.bfloat16), ahead)
-        before = pltpu.roll(jnp.max(rank, axis=1, keepdims=True) + jnp.zeros_like(rank), 1, 0)
-        odd = iota(rank.shape, 0) % 2 == 1
-        p_rank[: zs * cols_n] = rank + jnp.where(odd, before, 0.0)
+                hit = jnp.minimum(hit, 1.0)
+                for f in range(stages):
+                    inside = jnp.logical_and(b >= starts[f], b < starts[f] + phases[f][0])
+                    p_need[pl.ds(p_at(f, d, c), 1)] = jnp.where(inside, hit, 0.0)
+        ranked(p_need, p_rank, stages * zs * cols_n)
 
     def need_s():
         for r in range(rows_n):
             wants = flat(nt(q_dense[r], p_dense[r]))
             for source in range(rows_n):
-                k, j = split_s(source, col)
-                hit = nn(wants, onehot(k, LANES)) * onehot(j, LANES, jnp.float32)
-                hit = jnp.sum(hit, axis=0, keepdims=True)
-                s_need[pl.ds(r * rows_n + source, 1)] = jnp.minimum(hit, 1.0)
-        square = rows_n * rows_n
-        s_rank[:square] = nn(s_need[:square].astype(jnp.bfloat16), ahead)
+                for half in range(2):
+                    k, j = split_s(source, z * 2 + half)
+                    hit = nn(wants, onehot(k, LANES)) * onehot(j, LANES, jnp.float32)
+                    hit = jnp.sum(hit, axis=0, keepdims=True)
+                    s_need[pl.ds(s_at(r, source, half), 1)] = jnp.minimum(hit, 1.0)
+        ranked(s_need, s_rank, rows_n * rows_n * 2)
 
     def picks(need, rank, base):
         chosen = jnp.logical_and(rank == (iota((LANES, LANES), 0) + 1).astype(jnp.float32), need > 0)
@@ -360,55 +387,68 @@
         values = (base + lane).astype(jnp.float32).astype(jnp.bfloat16)
         return nt(values, chosen)
 
+    def picked(need, rank, at):
+        entry = jnp.zeros((8, LANES), jnp.float32)
+        for half in range(2):
+            row_at = pl.ds(at + half, 1)
+            entry += picks(need[row_at], rank[row_at], half * slots)
+        return entry
+
     def make_lists():
-        made = jnp.zeros((8, LANES), jnp.float32)
-        for d in range(zs):
-            entry = jnp.zeros((8, LANES), jnp.float32)
-            for half in range(2):
-                at = d * cols_n + z * 2 + half
-                entry += picks(p_need[pl.ds(at, 1)], p_rank[pl.ds(at, 1)], half * slots)
-            made = jnp.where(height == d, entry, made)
-        for r in range(rows_n):
-            at = r * rows_n + row
-            entry = picks(s_need[pl.ds(at, 1)], s_rank[pl.ds(at, 1)], 0)
-            made = jnp.where(height == zs + r, entry, made)
-        lists[...] = made.astype(jnp.int32)
+        for n in range(lists.shape[0] // 8):
+            made = jnp.zeros((8, LANES), jnp.float32)
+            for at in range(8):
+                f, d = divmod(n * 8 + at, zs)
+                r = n * 8 + at - stages * zs
+                if f < stages:
+                    entry = picked(p_need, p_rank, p_at(f, d, z * 2))
+                elif r < rows_n:
+                    entry = picked(s_need, s_rank, s_at(r, row, 0))
+                else:
+                    continue
+                made = jnp.where(height == at, entry, made)
+            lists[n * 8 : n * 8 + 8] = made.astype(jnp.int32)
+        load_lists.start()
+
+    def make_flags():
         over = jnp.zeros((1, 1), jnp.float32)
         for d in range(zs):
-            most = jnp.max(p_rank[pl.ds(z * cols_n + d * 2 + 1, 1)], axis=1, keepdims=True)
-            over = jnp.maximum(over, jnp.where(d == z, 0.0, most - p_cap))
+            for f in range(stages):
+                most = jnp.max(p_rank[pl.ds(p_at(f, z, d * 2 + 1), 1)], axis=1, keepdims=True)
+                over = jnp.maximum(over, jnp.where(d == z, 0.0, most - caps[f]))
         for r in range(rows_n):
-            most = jnp.max(s_rank[pl.ds(row * rows_n + r, 1)], axis=1, keepdims=True)
+            most = jnp.max(s_rank[pl.ds(s_at(row, r, 1), 1)], axis=1, keepdims=True)
             over = jnp.maximum(over, jnp.where(r == row, 0.0, most - s_cap))
         flags[row, col] = (over + jnp.zeros((8, LANES), jnp.float32)).astype(jnp.int32)
+        flag_steps[0]()
 
     def make_codes():
-        p_at = jnp.zeros((tile_rows, LANES), jnp.float32)
+        p_sum = jnp.zeros((tile_rows, LANES), jnp.float32)
         for c in range(cols_n):
             a, k = split(0, row, c)
-            at = z * cols_n + c
-            own = (c % 2 * slots + 1 + lanes).astype(jnp.float32)
-            far = 2 * slots + c // 2 * p_cap + p_rank[pl.ds(at, 1)]
-            far = jnp.where(p_need[pl.ds(at, 1)] > 0, far, 0.0)
-            place = jnp.where(c // 2 == z, own, far)
-            p_at += nt(
+            place = (c % 2 * slots + 1 + lanes).astype(jnp.float32)
+            far = jnp.zeros((1, LANES), jnp.float32)
+            for f in range(stages):
+                at = pl.ds(p_at(f, z, c), 1)
+                spot = bases[f] + c // 2 * caps[f] + p_rank[at]
+                far = far + jnp.where(p_need[at] > 0, spot, 0.0)
+            place = jnp.where(c // 2 == z, place, far)
+            p_sum += nt(
                 onehot(a, tile_rows, jnp.float32) * place, onehot(k, LANES, jnp.float32), exact
             )
-        s_at = jnp.zeros((LANES, LANES), jnp.float32)
+        s_sum = jnp.zeros((LANES, LANES), jnp.float32)
         for r in range(rows_n):
             k, j = split_s(r, col)
-            at = row * rows_n + r
-            own = (1 + lanes).astype(jnp.float32)
-            far = slots + r * s_cap + s_rank[pl.ds(at, 1)]
-            far = jnp.where(s_need[pl.ds(at, 1)] > 0, far, 0.0)
-            place = jnp.where(r == row, own, far)
-            s_at += nt(onehot(j, LANES, jnp.float32) * place, onehot(k, LANES, jnp.float32), exact)
+            at = pl.ds(s_at(row, r, core), 1)
+            far = jnp.where(s_need[at] > 0, slots + r * s_cap + s_rank[at], 0.0)
+            place = jnp.where(r == row, (1 + lanes).astype(jnp.float32), far)
+            s_sum += nt(onehot(j, LANES, jnp.float32) * place, onehot(k, LANES, jnp.float32), exact)
         a, j = split(1, row, col)
         unit = onehot(lanes, LANES)
         q_row_hot = nt(unit, onehot(a, tile_rows))[:slots]
         q_col_hot = nt(unit, onehot(j, LANES))[:slots]
-        p_for = nn(q_row_hot, p_at, exact)
-        s_for = nn(q_col_hot, s_at, exact)
+        p_for = nn(q_row_hot, p_sum, exact)
+        s_for = nn(q_col_hot, s_sum, exact)
         match = jnp.where(jnp.logical_and(p_for > 0, s_for > 0), 1.0, 0.0)
         value = (p_for - 1) * CODE + (s_for - 1)
         rank = nn(match.astype(jnp.bfloat16), ahead) * match
@@ -421,166 +461,217 @@
             here = jnp.sum(here, axis=1, keepdims=True)
             return jnp.where(iota(made.shape, 1) == n, here, made)
 
-        made = lax.fori_loop(0, LANES, place_one, jnp.zeros((slots, LANES), jnp.float32))
+        made = jnp.zeros((slots, LANES), jnp.float32)
+        made = lax.fori_loop(0, LANES, place_one, made, unroll=8)
         codes[...] = made.astype(jnp.int32)
 
     load_lists = pltpu.make_async_copy(lists, lists_s, sem.at[2])
-
-    def before_three():
-        make_lists()
-        flag_steps[0]()
-        load_lists.start()
-
-    work = {
-        0: [meta_steps[1], meta_steps[2]],
-        1: [lambda: dense_rows(0), lambda: dense_rows(1)],
-        2: [lambda: dense_rows(2), lambda: dense_rows(3), dense_s],
-        3: [need_p],
-        4: [need_s, before_three],
-        5: [flag_steps[1], make_codes],
-        6: [flag_steps[2]],
-    }
-
-    def relay(k):
-        for part in range(parts):
-            now = k * parts + part
-            for way in range(2):
-
-                @pl.when(sends[way])
-                def _():
-                    copy(way, k, part).wait_recv()
-                    if now >= depth:
-                        copy(way, *steps[now - depth]).wait_send()
-                    copy(way, k, part).start()
 
     groups = 4
     group = slots // groups
 
-    def pair_copy(n):
-        where = p_pair.at[pl.ds(core * slots + n * group, group)]
-        return remote(where, where, pair_send.at[n], pair_recv.at[n], partner)
-
-    def pair_got(n):
-        where = p_pair.at[pl.ds((1 - core) * slots + n * group, group)]
-        return remote(where, where, pair_send.at[n], pair_recv.at[n], partner)
-
-    relay(0)
+    def pair_copy(f, n, half):
+        where = p_pair[f].at[pl.ds(half * slots + n * group, group)]
+        return remote(where, where, pair_send.at[f, n], pair_recv.at[f, n], partner)
+
+    def s_pair_copy(half):
+        where = s_pair.at[pl.ds(half * slots, slots)]
+        return remote(where, where, s_swap.at[0], s_swap.at[1], partner)
+
+    def chip(n):
+        return lax.rem(z + n + 1, zs)
+
+    def p_copy(f, n):
+        device = {"row": row, "col": chip(n) * 2 + core}
+        where = p_recv[f].at[z, core]
+        return remote(p_pack[f].at[n], where, p_send.at[f, n], p_got.at[f, z], device)
+
+    def p_arrival(f, n):
+        where = p_recv[f].at[chip(n), core]
+        return remote(p_pack[f].at[n], where, p_send.at[f, n], p_got.at[f, chip(n)], partner)
+
+    def p_pass(f, n, half):
+        where = p_recv[f].at[chip(n), half]
+        return remote(where, where, pass_send.at[f, n], pass_recv.at[f, chip(n)], partner)
+
+    def s_copy(n):
+        where = s_recv.at[row, core]
+        return remote(s_pack.at[n], where, s_send.at[n], s_got.at[row], col_mates[n])
+
+    def s_arrival(n):
+        source = col_mates[n]["row"]
+        where = s_recv.at[source, core]
+        return remote(s_pack.at[n], where, s_send.at[n], s_got.at[source], partner)
+
+    def s_pass(n, half):
+        source = col_mates[n]["row"]
+        where = s_recv.at[source, half]
+        return remote(where, where, s_pass_send.at[n], s_pass_recv.at[source], partner)
+
+    def pack_p(f):
+        for n in range(groups):
+            pair_copy(f, n, 1 - core).wait_recv()
+        half = caps[f] // 2
+        for n in range(zs - 1):
+
+            def fill(t, carry, n=n):
+                at = lists_s[f * zs + chip(n), core * half + t]
+                p_pack[f][n, t] = p_pair[f][jnp.clip(at, 0, 2 * slots - 1)]
+                return carry
+
+            lax.fori_loop(0, half, fill, 0, unroll=5)
+            if f == stages - 1 or n == 0:
+                p_copy(f, n).start()
+
+    def pack_s():
+        s_pair_copy(1 - core).wait_recv()
+        half = s_cap // 2
+        for n in range(rows_n - 1):
+
+            def fill(t, carry, n=n):
+                at = lists_s[stages * zs + col_mates[n]["row"], core * half + t]
+                s_pack[n, t] = s_pair[jnp.clip(at, 0, 2 * slots - 1)]
+                return carry
+
+            lax.fori_loop(0, half, fill, 0, unroll=2)
+
+    def start_swap():
+        load_s.wait()
+        s_pair_copy(core).start()
+
+    ready = phases[0][1]
+    idle = [lambda: None]
+    ready = phases[0][1]
+    work = {
+        0: [meta_steps[1]] + idle * 3 + [start_swap],
+        1: [meta_steps[2]] + [functools.partial(dense_rows, r) for r in range(rows_n)],
+        2: [dense_s, idle[0], need_p],
+        3: [need_s, idle[0], make_lists],
+        ready: [load_lists.wait, lambda: pack_p(0), make_flags],
+        ready + 1: [p_copy(0, 1).start, flag_steps[1], make_codes],
+        ready + 2: [flag_steps[2], idle[0], pack_s],
+        ready + 3: [p_copy(0, 2).start],
+    }
+
+    def relay(n, part):
+        f, k = pieces[n]
+        now = steps.index((f, k, part))
+        for way in range(2):
+
+            @pl.when(sends[way])
+            def _():
+                copy(way, f, k, part).wait_recv()
+                if now >= depth:
+                    copy(way, *steps[now - depth]).wait_send()
+                copy(way, f, k, part).start()
+
+    for n in range(LAG):
+        for part in range(phases[pieces[n][0]][2]):
+            relay(n, part)
     load_left.wait()
-    for k in range(chunks):
-        if k < chunks - 1:
-            relay(k + 1)
+    for n, (f, k) in enumerate(pieces):
         for way in range(2):
 
             @pl.when(jnp.logical_not(sends[way]))
             def _():
-                for part in range(parts):
-                    copy(way, k, part).wait_recv()
-
-        def block(slot, carry, k=k):
-            raw = lax.dot_general(
-                left[ids[slot] >> bits, :, pl.ds(k * wide, wide)],
-                right[k][ids[slot] & (tile_cols - 1)],
-                (((1,), (1,)), ((), ())),
-                preferred_element_type=jnp.float32,
-            )
+                for part in range(phases[f][2]):
+                    copy(way, f, k, part).wait_recv()
+
+        if n == len(pieces) - 1:
+            for one in range(rows_n - 1):
+                s_copy(one).start()
+        wide = right[f][k].shape[2]
+        ends = k == phases[f][1] - 1
+
+        def blocks(step, carry, f=f, k=k, wide=wide, ends=ends):
+            slot = [step * BATCH + one for one in range(BATCH)]
+            b = [(ids[at] & (tile_cols - 1)) - starts[f] for at in slot]
+            raw = [
+                lax.dot_general(
+                    left[ids[at] >> bits, :, pl.ds(k * wide, wide)],
+                    right[f][k][jnp.clip(where, 0, phases[f][0] - 1)],
+                    (((1,), (1,)), ((), ())),
+                    preferred_element_type=jnp.float32,
+                )
+                for at, where in zip(slot, b)
+            ]
             if k > 0:
-                raw = raw + total[slot]
-            if k < chunks - 1:
-                total[slot] = raw
-            else:
-                raw = jnp.where(slot < count[0], raw, 0.0)
-                p_pair[core * slots + slot] = raw.astype(p_pair.dtype)
+                raw = [one + total[at] for one, at in zip(raw, slot)]
+            if not ends:
+                for one, at in zip(raw, slot):
+                    total[at] = one
+                return carry
+            made = []
+            for one, at, where in zip(raw, slot, b):
+                inside = jnp.logical_and(where >= 0, where < phases[f][0])
+                inside = jnp.logical_and(inside, at < count[0])
+                other = 0.0
+                if f > 0:
+                    other = p_pair[f - 1][core * slots + at].astype(jnp.float32)
+                made.append(jnp.where(inside, one, other).astype(p_pair[f].dtype))
+            for one, at in zip(made, slot):
+                p_pair[f][core * slots + at] = one
             return carry
 
-        if k < chunks - 1:
-            lax.fori_loop(0, slots, block, 0, unroll=4)
-            for one in work.get(k, []):
-                one()
+        todo = list(work.get(n, []))
+        later = n + LAG
+        if later < len(pieces):
+            pulls = [functools.partial(relay, later, p) for p in range(phases[pieces[later][0]][2])]
         else:
-            for n in range(groups):
-                lax.fori_loop(n * group, (n + 1) * group, block, 0, unroll=4)
-                pair_copy(n).start()
-
-    density_out = pltpu.make_async_copy(p_pair.at[pl.ds(core * slots, slots)], density, done.at[0])
+            pulls = []
+        turns = groups if ends else max(len(pulls), len(todo), 1)
+        batches = slots // BATCH
+        for turn in range(turns):
+            if turn < len(pulls):
+                pulls[turn]()
+            low, high = batches * turn // turns, batches * (turn + 1) // turns
+            lax.fori_loop(low, high, blocks, 0)
+            if ends:
+                pair_copy(f, turn, core).start()
+            if turn < len(todo):
+                todo[turn]()
+        for one in pulls[turns:] + todo[turns:]:
+            one()
+
+    final = p_pair[-1]
+    density_out = pltpu.make_async_copy(final.at[pl.ds(core * slots, slots)], density, done.at[0])
     density_out.start()
-    load_s.wait()
-    load_lists.wait()
-
-    def s_copy(n):
-        r = col_mates[n]["row"]
-        return remote(s_pack.at[n], s_recv.at[row], s_send.at[n], s_got.at[row], col_mates[n])
-
-    def s_arrival(n):
-        source = col_mates[n]["row"]
-        return remote(s_pack.at[n], s_recv.at[source], s_send.at[n], s_got.at[source], col_mates[n])
-
-    for n in range(groups):
-        pair_got(n).wait_recv()
-    pair_out = pltpu.make_async_copy(p_pair, p_pair_out, done.at[1])
-    pair_out.start()
-
-    def chip(n):
-        return lax.rem(z + n + 1, zs)
-
-    def p_copy(n):
-        device = {"row": row, "col": chip(n) * 2 + core}
-        return remote(p_pack.at[n], p_recv.at[z, core], p_send.at[n], p_got.at[z], device)
-
-    def p_arrival(n):
-        where = p_recv.at[chip(n), core]
-        return remote(p_pack.at[n], where, p_send.at[n], p_got.at[chip(n)], partner)
-
-    def p_pass(n, half):
-        where = p_recv.at[chip(n), half]
-        return remote(where, where, pass_send.at[n], pass_recv.at[chip(n)], partner)
-
-    for n in range(zs - 1):
-        start = core * (p_cap // 2)
-
-        def fill(t, carry, n=n):
-            at = lists_s[chip(n), core * (p_cap // 2) + t]
-            p_pack[n, t] = p_pair[jnp.clip(at, 0, 2 * slots - 1)]
-            return carry
-
-        lax.fori_loop(0, p_cap // 2, fill, 0, unroll=2)
-        p_copy(n).start()
-    for n in range(rows_n - 1):
-
-        def fill_s(t, carry, n=n):
-            at = lists_s[zs + col_mates[n]["row"], t]
-            s_pack[n, t] = s_own[jnp.clip(at, 0, s_own.shape[0] - 1)]
-            return carry
-
-        lax.fori_loop(0, s_cap, fill_s, 0, unroll=2)
-        s_copy(n).start()
-
+    pack_p(stages - 1)
+    pair_out = pltpu.make_async_copy(final, p_pair_out, done.at[1])
     flags_go = pltpu.make_async_copy(flags, flags_out, done.at[2])
     meta_go = pltpu.make_async_copy(meta, meta_out, done.at[3])
-    flags_go.start()
-    meta_go.start()
+    for one in (pair_out, flags_go, meta_go):
+        one.start()
     for way in range(2):
 
         @pl.when(sends[way])
         def _():
-            for k, part in steps[-depth:]:
-                copy(way, k, part).wait_send()
-
-    for n in range(groups):
-        pair_copy(n).wait_send()
-    for n in range(zs - 1):
-        p_arrival(n).wait_recv()
-        p_pass(n, core).start()
+            for step in steps[-depth:]:
+                copy(way, *step).wait_send()
+
+    s_pair_copy(core).wait_send()
+    for f in range(stages):
+        for n in range(groups):
+            pair_copy(f, n, core).wait_send()
+    for f in range(stages):
+        if f == stages - 1:
+            for n in range(rows_n - 1):
+                s_arrival(n).wait_recv()
+                s_pass(n, core).start()
+        for n in range(zs - 1):
+            p_arrival(f, n).wait_recv()
+            p_pass(f, n, core).start()
     for n in range(rows_n - 1):
-        s_arrival(n).wait_recv()
+        s_pass(n, 1 - core).wait_recv()
+        s_pass(n, core).wait_send()
         s_copy(n).wait_send()
-    for n in range(zs - 1):
-        p_pass(n, 1 - core).wait_recv()
-        p_pass(n, core).wait_send()
-        p_copy(n).wait_send()
-    density_out.wait()
-    pair_out.wait()
-    flags_go.wait()
-    meta_go.wait()
+    for f in range(stages):
+        for n in range(zs - 1):
+            p_pass(f, n, 1 - core).wait_recv()
+            p_pass(f, n, core).wait_send()
+            p_copy(f, n).wait_send()
+    for one in (density_out, pair_out, flags_go, meta_go):
+        one.wait()
 
 
 def panel_density(ids, counts, coeffs, s_own, rows_n, cols_n):
@@ -588,11 +679,8 @@
     orbitals = coeffs.shape[1]
     blocks = coeffs.reshape(-1, 128, orbitals)
     tile_rows = blocks.shape[0]
-    tile_cols = tile_rows * rows_n // cols_n
-    chunks = max(1, orbitals // CHUNK)
-    parts = max(1, tile_cols // (2 * PIECE))
     zs = cols_n // 2
-    half = P_CAP // 2
+    stages = len(PHASES)
     kind = coeffs.dtype
     block = (128, 128)
     smem, vmem = pl.BlockSpec(memory_space=pltpu.SMEM), pl.BlockSpec(memory_space=pltpu.VMEM)
@@ -600,60 +688,67 @@
     rows = [jnp.pad(one[None], ((0, 0), (0, LANES - slots)), constant_values=-1) for one in ids]
     table = (rows_n, cols_n, 8, LANES)
     sems = pltpu.SemaphoreType.DMA
-    floats = [
-        pltpu.VMEM((rows_n, LANES, tile_rows), jnp.bfloat16),
-        pltpu.VMEM((rows_n, LANES, tile_rows), jnp.bfloat16),
-        pltpu.VMEM((rows_n, tile_rows, LANES), jnp.bfloat16),
-        pltpu.VMEM((LANES, LANES), jnp.bfloat16),
-        pltpu.VMEM((zs * cols_n + 8, LANES), jnp.float32),
-        pltpu.VMEM((zs * cols_n + 8, LANES), jnp.float32),
-        pltpu.VMEM((rows_n * rows_n + 8, LANES), jnp.float32),
-        pltpu.VMEM((rows_n * rows_n + 8, LANES), jnp.float32),
+    steps = sum(chunks * parts for _, chunks, parts, _ in PHASES)
+    p_rows, s_rows = stages * zs * cols_n + 8, rows_n * rows_n * 2 + 8
+    list_rows = -(-(stages * zs + rows_n) // 8) * 8
+    mates = cols_n + rows_n - 2
+    panels = [
+        pltpu.VMEM((wide, 128, orbitals // chunks), kind)
+        for wide, chunks, _, _ in PHASES
+        for _ in range(chunks)
     ]
     return pl.pallas_call(
-        functools.partial(panel_kernel, rows_n, cols_n, chunks, parts, DEPTH),
-        out_shape=(
+        functools.partial(panel_kernel, rows_n, cols_n, PHASES, DEPTH),
+        out_shape=[
             jax.ShapeDtypeStruct((slots,) + block, kind),
             jax.ShapeDtypeStruct((2 * slots,) + block, kind),
-            jax.ShapeDtypeStruct((zs, 2, half) + block, kind),
-            jax.ShapeDtypeStruct((rows_n, S_CAP) + block, kind),
+            jax.ShapeDtypeStruct((rows_n, 2, S_CAP // 2) + block, kind),
             jax.ShapeDtypeStruct((slots, LANES), jnp.int32),
             jax.ShapeDtypeStruct((8, slots), jnp.int32),
             jax.ShapeDtypeStruct(table, jnp.int32),
             jax.ShapeDtypeStruct(table, jnp.int32),
-        ),
+        ]
+        + [jax.ShapeDtypeStruct((zs, 2, cap // 2) + block, kind) for _, _, _, cap in PHASES],
         in_specs=[smem, smem] + [vmem, smem] * 3 + [anywhere] * 2,
-        out_specs=[anywhere] * 4 + [vmem] * 2 + [anywhere] * 2,
-        scratch_shapes=[pltpu.VMEM((tile_cols, 128, orbitals // chunks), kind)] * chunks
+        out_specs=[anywhere] * 3 + [vmem] * 2 + [anywhere] * (2 + stages),
+        scratch_shapes=panels
+        + [pltpu.VMEM((2 * slots,) + block, kind)] * stages
+        + [pltpu.VMEM((zs - 1, cap // 2) + block, kind) for _, _, _, cap in PHASES]
         + [
             pltpu.VMEM(blocks.shape, kind),
             pltpu.VMEM((slots,) + block, jnp.float32),
             pltpu.VMEM((2 * slots,) + block, kind),
-            pltpu.VMEM((slots,) + block, kind),
-            pltpu.VMEM((zs - 1, half) + block, kind),
-            pltpu.VMEM((rows_n - 1, S_CAP) + block, kind),
+            pltpu.VMEM((rows_n - 1, S_CAP // 2) + block, kind),
             pltpu.VMEM(table, jnp.int32),
             pltpu.VMEM(table, jnp.int32),
-        ]
-        + floats
-        + [
-            pltpu.VMEM((8, LANES), jnp.int32),
-            pltpu.SMEM((8, LANES), jnp.int32),
-            sems((2, chunks * parts)),
-            sems((2, chunks * parts)),
+            pltpu.VMEM((rows_n, LANES, tile_rows), jnp.bfloat16),
+            pltpu.VMEM((rows_n, LANES, tile_rows), jnp.bfloat16),
+            pltpu.VMEM((rows_n, tile_rows, LANES), jnp.bfloat16),
+            pltpu.VMEM((LANES, LANES), jnp.bfloat16),
+            pltpu.VMEM((p_rows, LANES), jnp.float32),
+            pltpu.VMEM((p_rows, LANES), jnp.float32),
+            pltpu.VMEM((s_rows, LANES), jnp.float32),
+            pltpu.VMEM((s_rows, LANES), jnp.float32),
+            pltpu.VMEM((list_rows, LANES), jnp.int32),
+            pltpu.SMEM((list_rows, LANES), jnp.int32),
+            sems((2, steps)),
+            sems((2, steps)),
             sems((3,)),
-            sems((cols_n + rows_n - 2,)),
+            sems((mates,)),
             sems((cols_n + rows_n,)),
-            sems((cols_n + rows_n - 2,)),
+            sems((mates,)),
             sems((cols_n + rows_n,)),
-            sems((4,)),
-            sems((4,)),
-            sems((zs - 1,)),
-            sems((zs,)),
-            sems((zs - 1,)),
-            sems((zs,)),
+            sems((stages, 4)),
+            sems((stages, 4)),
+            sems((stages, zs - 1)),
+            sems((stages, zs)),
+            sems((stages, zs - 1)),
+            sems((stages, zs)),
             sems((rows_n - 1,)),
             sems((rows_n,)),
+            sems((rows_n - 1,)),
+            sems((rows_n,)),
+            sems((2,)),
             sems((4,)),
         ],
         compiler_params=pltpu.CompilerParams(
@@ -662,14 +757,15 @@
     )(ids[0], counts[0], rows[0], counts[0], rows[1], counts[1], rows[2], counts[2], blocks, s_own)
 
 
-def packed_kernel(codes, counts, p_pair, p_recv, s_own, s_recv, out, left, right, sem):
-    near, s_near = p_pair.shape[0], s_own.shape[0]
-    loads = [
-        pltpu.make_async_copy(p_pair, left.at[pl.ds(0, near)], sem.at[0]),
-        pltpu.make_async_copy(p_recv, left.at[pl.ds(near, p_recv.shape[0])], sem.at[1]),
-        pltpu.make_async_copy(s_own, right.at[pl.ds(0, s_near)], sem.at[2]),
-        pltpu.make_async_copy(s_recv, right.at[pl.ds(s_near, s_recv.shape[0])], sem.at[3]),
-    ]
+def packed_kernel(codes, counts, *refs):
+    sources, (out, left, right, sem) = refs[:-4], refs[-4:]
+    loads = []
+    for target, group in ((left, sources[:-2]), (right, sources[-2:])):
+        at = 0
+        for source in group:
+            where = target.at[pl.ds(at, source.shape[0])]
+            loads.append(pltpu.make_async_copy(source, where, sem.at[len(loads)]))
+            at += source.shape[0]
     for load in loads:
         load.start()
     for load in loads:
@@ -690,22 +786,22 @@
     lax.fori_loop(0, out.shape[0], slot, 0)
 
 
-def packed_product(codes, counts, p_pair, p_recv, s_own, s_recv):
-    p_recv = p_recv.reshape(-1, 128, 128)
-    s_recv = s_recv.reshape(-1, 128, 128)
+def packed_product(codes, counts, p_parts, s_parts):
+    p_parts = [part.reshape(-1, 128, 128) for part in p_parts]
+    s_parts = [part.reshape(-1, 128, 128) for part in s_parts]
+    sizes = [sum(part.shape[0] for part in parts) for parts in (p_parts, s_parts)]
+    kind = s_parts[0].dtype
+    many = len(p_parts) + len(s_parts)
     return pl.pallas_call(
         packed_kernel,
         out_shape=jax.ShapeDtypeStruct((codes.shape[0], 128, 128), jnp.float32),
         in_specs=[pl.BlockSpec(memory_space=pltpu.SMEM)] * 2
-        + [pl.BlockSpec(memory_space=pl.ANY)] * 4,
+        + [pl.BlockSpec(memory_space=pl.ANY)] * many,
         out_specs=pl.BlockSpec(memory_space=pltpu.VMEM),
-        scratch_shapes=[
-            pltpu.VMEM((p_pair.shape[0] + p_recv.shape[0], 128, 128), p_pair.dtype),
-            pltpu.VMEM((s_own.shape[0] + s_recv.shape[0], 128, 128), s_own.dtype),
-            pltpu.SemaphoreType.DMA((4,)),
-        ],
+        scratch_shapes=[pltpu.VMEM((size, 128, 128), kind) for size in sizes]
+        + [pltpu.SemaphoreType.DMA((many,))],
         compiler_params=pltpu.CompilerParams(vmem_limit_bytes=40 * MIB),
-    )(codes, counts, p_pair, p_recv, s_own, s_recv)
+    )(codes, counts, *p_parts, *s_parts)
 
 
 def blocks_kernel(rows_n, cols_n, parts, p_own, s_own, p_all, s_all, *sems):
@@ -933,9 +1029,10 @@
         p_all, s_all = gather_blocks(p_own, s_own, rows_n, cols_n)
         return block_product(codes, counts, p_own, s_own, p_all, s_all)
 
-    if rows_n == 4 and tile_cols * cols_n == LANES and max(p_max, s_max, q_max) <= LANES // 2:
+    fits = tile_cols * cols_n == LANES and sum(one[0] for one in PHASES) == tile_cols
+    if rows_n == 4 and fits and p_max == s_max == q_max == LANES // 2:
         counts = (p_count[0], q_count[0], s_count[0])
-        p_own, p_pair, p_recv, s_recv, codes, pairs, over, meta = panel_density(
+        p_own, p_pair, s_recv, codes, pairs, over, meta, *p_recv = panel_density(
             (p_ids, q_ids, s_ids), counts, coeffs, s_own, rows_n, cols_n
         )
 
@@ -946,7 +1043,7 @@
             return whole(p_codes, s_codes, p_own)
 
         def packed():
-            return packed_product(codes, pairs, p_pair, p_recv, s_own, s_recv)
+            return packed_product(codes, pairs, [p_pair, *p_recv], [s_own, s_recv])
 
         product = lax.cond(jnp.max(over) > 0, full, packed)
     else:

time: 251 us -> 207 us (0.82)
  the two profiles are of different devices: /device:TPU:31 before, /device:TPU:11 now
where the time goes in v3:
time: 207 us; the launch traced here: 206 us
  Pallas kernels  194 us (94%)
  local copies, waits for them, and re-layouts  6.72 us (3%)
  between operations  3.26 us (2%)
    pallas_call x1, Pallas kernels, panel_density(): pl.pallas_call(functools.partial(panel_kernel, rows_n, cols_n, PHASES, DE...  182 us
    pallas_call x1, Pallas kernels, packed_product(): pl.pallas_call(packed_kernel, out_shape=jax.ShapeDtypeStruct((codes.shape...  12.5 us

profile of v3, /device:TPU:11, one launch (start us, length us, event | category | flops | bytes accessed | tf_op | source)
XLA Modules:
  0.0 206.1 jit_solution(7581880507821581350)
XLA Ops:
  2.6 1.2 pad.12.refs_6_
  3.8 1.2 pad.11.refs_4_
  5.0 1.2 pad.10.refs_2_
  6.1 0.0 copy-start.1
  6.1 0.0 copy-start.2
  6.1 181.7 %shard_map.95 = (bf16[64,128,128]{2,1,0:T(8,128)(2,1)}, bf16[128,128,128]{2,1,0:T(8,128)(2,1)}, bf16[4,2,22,128,128]{4,3,2,1,0:T(8,128)(2,1)}, s32[64,128]{1,0:T...) custom-call(s32[64]{0:T(128)} %bitcast.64, ...), custom_call_target="tpu_custom_call" | custom-call | tf_op jit(solution)/shard_map/pallas_call | solution.py:700
  187.8 1.6 reduce_max.27
  190.1 0.0 copy-done.1
  190.1 0.0 copy-done.2
  190.1 12.8 %conditional.1 = (f32[1,1,64,128,128]{4,3,2,1,0:T(8,128)}) conditional(s32[]{:T(128)} %convert_element_type.13, (bf16[4,2,15,128,128]{4,3,2,1,0:T(8,128)(2,1)}, bf16[4,2,10,128,128]{4,3,2,1,0:T(8,128)(2,1)}, bf16[4,2,22,128,128]{4,3,2,1,0:T(8,128)(2,1)}, s32[64,128]{1,0:T(8,128)S(1)}, s32[8,64]{1,0:T(8,128)S(1)}, ...), branch_computations={%region_1.2_spmd, %region_2.8_spmd} | conditional | flops 9533291 | bytes 34825320 | solution.py:1048
  190.1 12.5 %branch_0_fun.1 = f32[64,128,128]{2,1,0:T(8,128)} custom-call(s32[64,128]{1,0:T(8,128)S(1)} %get-tuple-element.29.codes, s32[8,64]{1,0:T(8,128)S(1)} %get-tuple-element.30.counts, bf16[128,128,128]{2,1,0:T(8,128)(2,1)} %get-tuple-element.31.refs_0_, bf16[120,128,128]{2,1,0:T(8,128)(2,1)} %bitcast.55, bf16[80,128,128]{2,1,0:T(8,128)(2,1)} %bitcast.56, ...), custom_call_target="tpu_custom_call" | custom-call | tf_op jit(solution)/shard_map/cond/branch_0_fun/pallas_call | solution.py:795
  202.9 3.2 %copy.35 = bf16[1,1,64,128,128]{4,3,2,1,0:T(8,128)(2,1)} copy(bf16[1,1,64,128,128]{4,3,2,1,0:T(8,128)(2,1)} %bitcast.50) | data formatting | bytes 4194304
Async XLA Ops:
  6.1 183.9 %copy-start.1 = (bf16[1,1,64,128,128]{4,3,2,1,0:T(8,128)(2,1)S(1)}, bf16[1,1,64,128,128]{4,3,2,1,0:T(8,128)(2,1)}, u32[]{:S(2)}) copy-start(bf16[1,1,64,128,128]{4,3,2,1,0:T(8,128)(2,1)} %param.13) | copy-start | bytes 6291460
  6.1 183.9 %copy-start.2 = (s32[1,1,64]{2,1,0:T(1,128)S(1)}, s32[1,1,64]{2,1,0:T(1,128)}, u32[]{:S(2)}) copy-start(s32[1,1,64]{2,1,0:T(1,128)} %param.16) | copy-start | bytes 772

commit v4 on v3

--- a/solution.py
+++ b/solution.py
@@ -10,12 +10,13 @@
 MESH = pl.DeviceIdType.MESH
 MIB = 1 << 20
 DEPTH = 3
-BATCH = 8
+BATCHES = (4, 8)
+RING = 16
 LANES = 128
 CODE = 512
-PHASES = ((10, 4, 5, 30), (6, 4, 3, 20))
+PHASES = ((10, 4, 5, 28), (6, 4, 3, 18))
 LAG = 2
-S_CAP = 44
+S_CAP = 42
 
 
 def rows_kernel(rows_n, cols_n, coeffs, out, send, recv):
@@ -165,9 +166,9 @@
 def panel_kernel(rows_n, cols_n, phases, depth, *refs):
     stages = len(phases)
     ids, count, p_row, p_live, q_row, q_live, s_row, s_live, coeffs, s_in = refs[:10]
-    density, p_pair_out, s_recv, codes, counts, flags_out, meta_out = refs[10:17]
-    p_recv = refs[17 : 17 + stages]
-    refs = refs[17 + stages :]
+    p_pair_out, s_recv, codes, counts, flags_out, meta_out = refs[10:16]
+    p_recv = refs[16 : 16 + stages]
+    refs = refs[16 + stages :]
     right = []
     for _, chunks, _, _ in phases:
         right.append(refs[:chunks])
@@ -519,7 +520,7 @@
                 p_pack[f][n, t] = p_pair[f][jnp.clip(at, 0, 2 * slots - 1)]
                 return carry
 
-            lax.fori_loop(0, half, fill, 0, unroll=5)
+            lax.fori_loop(0, half, fill, 0)
             if f == stages - 1 or n == 0:
                 p_copy(f, n).start()
 
@@ -533,7 +534,7 @@
                 s_pack[n, t] = s_pair[jnp.clip(at, 0, 2 * slots - 1)]
                 return carry
 
-            lax.fori_loop(0, half, fill, 0, unroll=2)
+            lax.fori_loop(0, half, fill, 0)
 
     def start_swap():
         load_s.wait()
@@ -583,8 +584,8 @@
         wide = right[f][k].shape[2]
         ends = k == phases[f][1] - 1
 
-        def blocks(step, carry, f=f, k=k, wide=wide, ends=ends):
-            slot = [step * BATCH + one for one in range(BATCH)]
+        def blocks(step, carry, f=f, k=k, wide=wide, ends=ends, batch=BATCHES[f]):
+            slot = [step * batch + one for one in range(batch)]
             b = [(ids[at] & (tile_cols - 1)) - starts[f] for at in slot]
             raw = [
                 lax.dot_general(
@@ -620,7 +621,7 @@
         else:
             pulls = []
         turns = groups if ends else max(len(pulls), len(todo), 1)
-        batches = slots // BATCH
+        batches = slots // BATCHES[f]
         for turn in range(turns):
             if turn < len(pulls):
                 pulls[turn]()
@@ -634,8 +635,6 @@
             one()
 
     final = p_pair[-1]
-    density_out = pltpu.make_async_copy(final.at[pl.ds(core * slots, slots)], density, done.at[0])
-    density_out.start()
     pack_p(stages - 1)
     pair_out = pltpu.make_async_copy(final, p_pair_out, done.at[1])
     flags_go = pltpu.make_async_copy(flags, flags_out, done.at[2])
@@ -670,7 +669,7 @@
             p_pass(f, n, 1 - core).wait_recv()
             p_pass(f, n, core).wait_send()
             p_copy(f, n).wait_send()
-    for one in (density_out, pair_out, flags_go, meta_go):
+    for one in (pair_out, flags_go, meta_go):
         one.wait()
 
 
@@ -700,7 +699,6 @@
     return pl.pallas_call(
         functools.partial(panel_kernel, rows_n, cols_n, PHASES, DEPTH),
         out_shape=[
-            jax.ShapeDtypeStruct((slots,) + block, kind),
             jax.ShapeDtypeStruct((2 * slots,) + block, kind),
             jax.ShapeDtypeStruct((rows_n, 2, S_CAP // 2) + block, kind),
             jax.ShapeDtypeStruct((slots, LANES), jnp.int32),
@@ -710,7 +708,7 @@
         ]
         + [jax.ShapeDtypeStruct((zs, 2, cap // 2) + block, kind) for _, _, _, cap in PHASES],
         in_specs=[smem, smem] + [vmem, smem] * 3 + [anywhere] * 2,
-        out_specs=[anywhere] * 3 + [vmem] * 2 + [anywhere] * (2 + stages),
+        out_specs=[anywhere] * 2 + [vmem] * 2 + [anywhere] * (2 + stages),
         scratch_shapes=panels
         + [pltpu.VMEM((2 * slots,) + block, kind)] * stages
         + [pltpu.VMEM((zs - 1, cap // 2) + block, kind) for _, _, _, cap in PHASES]
@@ -757,49 +755,98 @@
     )(ids[0], counts[0], rows[0], counts[0], rows[1], counts[1], rows[2], counts[2], blocks, s_own)
 
 
-def packed_kernel(codes, counts, *refs):
-    sources, (out, left, right, sem) = refs[:-4], refs[-4:]
-    loads = []
-    for target, group in ((left, sources[:-2]), (right, sources[-2:])):
-        at = 0
-        for source in group:
-            where = target.at[pl.ds(at, source.shape[0])]
-            loads.append(pltpu.make_async_copy(source, where, sem.at[len(loads)]))
-            at += source.shape[0]
-    for load in loads:
-        load.start()
-    for load in loads:
-        load.wait()
-
-    def slot(q, carry):
+def packed_kernel(p_many, slots, codes, counts, *refs):
+    p_parts, s_parts = refs[:p_many], refs[p_many:-8]
+    out, density, left, right, own, flat, sem, done = refs[-8:]
+    core = lax.rem(lax.axis_index("col"), 2)
+    own_in = pltpu.make_async_copy(p_parts[0].at[pl.ds(core * slots, slots)], own, done.at[0])
+    own_out = pltpu.make_async_copy(own, density, done.at[1])
+    own_in.start()
+
+    def listed(q, at):
+        def one(n, at):
+            flat[at] = codes[q, n]
+            return at + 1
+
+        return lax.fori_loop(0, counts[0, q], one, at)
+
+    pairs = lax.fori_loop(0, slots, listed, 0)
+
+    def fetch(at):
+        spot = lax.rem(at, RING)
+        code = flat[at]
+        for side, (where, parts, ring) in enumerate(
+            ((lax.div(code, CODE), p_parts, left), (lax.rem(code, CODE), s_parts, right))
+        ):
+            low = 0
+            for part in parts:
+                high = low + part.shape[0]
+
+                @pl.when(jnp.logical_and(where >= low, where < high))
+                def _():
+                    pltpu.make_async_copy(
+                        part.at[where - low], ring.at[spot], sem.at[side, spot]
+                    ).start()
+
+                low = high
+
+    def ahead(at, carry):
+        fetch(at)
+        return carry
+
+    lax.fori_loop(0, jnp.minimum(pairs, RING), ahead, 0)
+    own_in.wait()
+    own_out.start()
+
+    def slot(q, at):
         def term(n, total):
-            code = codes[q, n]
-            return total + jnp.dot(
-                left[lax.div(code, CODE)],
-                right[lax.rem(code, CODE)],
-                preferred_element_type=jnp.float32,
-            )
-
-        out[q] = lax.fori_loop(0, counts[0, q], term, jnp.zeros((128, 128), jnp.float32))
-        return carry
-
-    lax.fori_loop(0, out.shape[0], slot, 0)
+            now = at + n
+            spot = lax.rem(now, RING)
+            pltpu.make_async_copy(p_parts[0].at[0], left.at[spot], sem.at[0, spot]).wait()
+            pltpu.make_async_copy(s_parts[0].at[0], right.at[spot], sem.at[1, spot]).wait()
+            total += jnp.dot(left[spot], right[spot], preferred_element_type=jnp.float32)
+
+            @pl.when(now + RING < pairs)
+            def _():
+                fetch(now + RING)
+
+            return total
+
+        many = counts[0, q]
+        out[q] = lax.fori_loop(0, many, term, jnp.zeros((128, 128), jnp.float32))
+        return at + many
+
+    lax.fori_loop(0, slots, slot, 0)
+    own_out.wait()
 
 
 def packed_product(codes, counts, p_parts, s_parts):
     p_parts = [part.reshape(-1, 128, 128) for part in p_parts]
     s_parts = [part.reshape(-1, 128, 128) for part in s_parts]
-    sizes = [sum(part.shape[0] for part in parts) for parts in (p_parts, s_parts)]
     kind = s_parts[0].dtype
+    slots = codes.shape[0]
     many = len(p_parts) + len(s_parts)
+    block = (128, 128)
     return pl.pallas_call(
-        packed_kernel,
-        out_shape=jax.ShapeDtypeStruct((codes.shape[0], 128, 128), jnp.float32),
+        functools.partial(packed_kernel, len(p_parts), slots),
+        out_shape=[
+            jax.ShapeDtypeStruct((slots,) + block, jnp.float32),
+            jax.ShapeDtypeStruct((slots,) + block, kind),
+        ],
         in_specs=[pl.BlockSpec(memory_space=pltpu.SMEM)] * 2
         + [pl.BlockSpec(memory_space=pl.ANY)] * many,
-        out_specs=pl.BlockSpec(memory_space=pltpu.VMEM),
-        scratch_shapes=[pltpu.VMEM((size, 128, 128), kind) for size in sizes]
-        + [pltpu.SemaphoreType.DMA((many,))],
+        out_specs=[
+            pl.BlockSpec(memory_space=pltpu.VMEM),
+            pl.BlockSpec(memory_space=pl.ANY),
+        ],
+        scratch_shapes=[
+            pltpu.VMEM((RING,) + block, kind),
+            pltpu.VMEM((RING,) + block, kind),
+            pltpu.VMEM((slots,) + block, kind),
+            pltpu.SMEM((codes.size,), jnp.int32),
+            pltpu.SemaphoreType.DMA((2, RING)),
+            pltpu.SemaphoreType.DMA((2,)),
+        ],
         compiler_params=pltpu.CompilerParams(vmem_limit_bytes=40 * MIB),
     )(codes, counts, *p_parts, *s_parts)
 
@@ -1032,7 +1079,7 @@
     fits = tile_cols * cols_n == LANES and sum(one[0] for one in PHASES) == tile_cols
     if rows_n == 4 and fits and p_max == s_max == q_max == LANES // 2:
         counts = (p_count[0], q_count[0], s_count[0])
-        p_own, p_pair, s_recv, codes, pairs, over, meta, *p_recv = panel_density(
+        p_pair, s_recv, codes, pairs, over, meta, *p_recv = panel_density(
             (p_ids, q_ids, s_ids), counts, coeffs, s_own, rows_n, cols_n
         )
 
@@ -1040,12 +1087,13 @@
             row, col = lax.axis_index("row"), lax.axis_index("col")
             p_codes = lax.dynamic_index_in_dim(meta, row, 0, False)[:, 0, :p_max]
             s_codes = lax.dynamic_index_in_dim(meta, col, 1, False)[:, 2, :s_max]
-            return whole(p_codes, s_codes, p_own)
+            p_own = lax.dynamic_slice_in_dim(p_pair, col % 2 * p_max, p_max)
+            return whole(p_codes, s_codes, p_own), p_own
 
         def packed():
             return packed_product(codes, pairs, [p_pair, *p_recv], [s_own, s_recv])
 
-        product = lax.cond(jnp.max(over) > 0, full, packed)
+        product, p_own = lax.cond(jnp.max(over) > 0, full, packed)
     else:
         p_codes = lax.all_gather(jnp.where(live(p_ids, p_count), p_ids, -1), "col")
         s_codes = lax.all_gather(jnp.where(live(s_ids, s_count), s_ids, -1), "row")

time: 207 us -> 195 us (0.942)
  Pallas kernels: 194 us -> 186 us
  local copies, waits for them, and re-layouts: 6.72 us -> 3.56 us
    pallas_call x1, Pallas kernels: 182 us -> 177 us  [panel_density(): pl.pallas_call(functools.partial(panel_kernel, rows_n, cols_n, PHASES, DE...]
    pallas_call x1, Pallas kernels: 12.5 us -> 9.31 us  [packed_product(): pl.pallas_call(functools.partial(packed_kernel, len(p_parts), slots), out...]
    unnamed x5 -> x4, local copies, waits for them, and re-layouts: 3.17 us -> 0.01 us
where the time goes in v4:
time: 195 us
  Pallas kernels  186 us (95%)
  local copies, waits for them, and re-layouts  3.56 us (2%)
  between operations  3.45 us (2%)
    pallas_call x1, Pallas kernels, panel_density(): pl.pallas_call(functools.partial(panel_kernel, rows_n, cols_n, PHASES, DE...  177 us
    pallas_call x1, Pallas kernels, packed_product(): pl.pallas_call(functools.partial(packed_kernel, len(p_parts), slots), out...  9.31 us

profile of v4, /device:TPU:11, one launch (start us, length us, event | category | flops | bytes accessed | tf_op | source)
XLA Modules:
  0.0 194.9 jit_solution(1742854582575508869)
XLA Ops:
  2.6 1.2 pad.12.refs_6_
  3.8 1.2 pad.11.refs_4_
  5.0 1.2 pad.10.refs_2_
  6.1 0.0 copy-start.1
  6.1 0.0 copy-start.2
  6.1 176.8 %shard_map.95 = (bf16[128,128,128]{2,1,0:T(8,128)(2,1)}, bf16[4,2,21,128,128]{4,3,2,1,0:T(8,128)(2,1)}, s32[64,128]{1,0:T(8,128)S(1)}, s32[8,64]{1,0:T(8,128)S(1...) custom-call(s32[64]{0:T(128)} %bitcast.61, ...), custom_call_target="tpu_custom_call" | custom-call | tf_op jit(solution)/shard_map/pallas_call | solution.py:699
  182.9 1.6 reduce_max.27
  185.1 0.0 copy-done.1
  185.1 0.0 copy-done.2
  185.2 9.6 %conditional.1 = ((f32[64,128,128]{2,1,0:T(8,128)}, bf16[64,128,128]{2,1,0:T(8,128)(2,1)})) conditional(s32[]{:T(128)} %convert_element_type.13, (bf16[4,2,14,128,128]{4,3,2,1,0:T(8,128)(2,1)}, bf16[4,2,9,128,128]{4,3,2,1,0:T(8,128)(2,1)}, bf16[4,2,21,128,128]{4,3,2,1,0:T(8,128)(2,1)}, s32[64,128]{1,0:T(8,128)S(1)}, s32[8,64]{1,0:T(8,128)S(1)}, ...), branch_computations={%region_1.2_spmd, %region_2.8_spmd} | conditional | flops 9533305 | bytes 39019792 | solution.py:1096
  185.2 9.3 %branch_0_fun.1 = (f32[64,128,128]{2,1,0:T(8,128)}, bf16[64,128,128]{2,1,0:T(8,128)(2,1)}) custom-call(s32[64,128]{1,0:T(8,128)S(1)} %get-tuple-element.37.codes, s32[8,64]{1,0:T(8,128)S(1)} %get-tuple-element.38.counts, bf16[128,128,128]{2,1,0:T(8,128)(2,1)} %get-tuple-element.39.refs_0_, bf16[112,128,128]{2,1,0:T(8,128)(2,1)} %bitcast.52, ...), custom_call_target="tpu_custom_call" | custom-call | tf_op jit(solution)/shard_map/cond/branch_0_fun/pallas_call | solution.py:830
Async XLA Ops:
  6.1 179.0 %copy-start.1 = (bf16[1,1,64,128,128]{4,3,2,1,0:T(8,128)(2,1)S(1)}, bf16[1,1,64,128,128]{4,3,2,1,0:T(8,128)(2,1)}, u32[]{:S(2)}) copy-start(bf16[1,1,64,128,128]{4,3,2,1,0:T(8,128)(2,1)} %param.13) | copy-start | bytes 6291460
  6.1 179.0 %copy-start.2 = (s32[1,1,64]{2,1,0:T(1,128)S(1)}, s32[1,1,64]{2,1,0:T(1,128)}, u32[]{:S(2)}) copy-start(s32[1,1,64]{2,1,0:T(1,128)} %param.16) | copy-start | bytes 772
